TPU v7x, 32 devices: a whole 2x2x4 slice. The times are simulated.
32 devices in a mesh: gx: 8 (over z, y), gy: 4 (over x, core).
Axes of the slice: x: 2, y: 2, z: 4, core: 2. Of those that a mesh axis runs over, the one named last changes fastest.
Arguments:
- charge_density: float32 [256, 256, 256], P('gx', 'gy'), may hold values from -5080 to 5140
Outputs:
- potential: float32 [256, 256, 256], P('gx', 'gy')
- energies: float32 [2], replicated
All inputs are finite; a program needn't handle non-finite values.
Results may differ from a plain program's by a relative error of at most 0.0003.
Values sent between devices are 32-bit elements.
No kernel may reach another device: no remote copies, remote signals or barrier semaphores. Data moves between devices by JAX's collectives and lax.ppermute only.
A program may use at most 192 MiB of HBM per device.

v0:
```python
import functools
import math

import jax
import jax.numpy as jnp
import numpy as np
from jax import lax
from jax.experimental import pallas as pl
from jax.experimental.pallas import tpu as pltpu
from jax.sharding import PartitionSpec as P

ORDER = 16
COUNT = ORDER + 1
PAIRS = 256
FACE_ROWS = 16
TERMS = 384
outer_ratio = 1.1
radius_scale = math.sqrt(3.0) / 2.0
F32 = jnp.float32
BF16 = jnp.bfloat16
EXACT = lax.Precision.HIGHEST


NN = (((1,), (0,)), ((), ()))
NT = (((1,), (1,)), ((), ()))
TN = (((0,), (0,)), ((), ()))


def pair_list():
    return [(p, q) for p in range(COUNT) for q in range(COUNT - p)]


def term_list():
    terms = [(0, l, m) for m in range(COUNT) for l in range(m, COUNT)]
    terms += [(1, l, m) for m in range(1, COUNT) for l in range(m, COUNT)]
    return terms


def split_np(table):
    import ml_dtypes

    high = table.astype(np.float32).astype(ml_dtypes.bfloat16)
    low = (table - high.astype(np.float64)).astype(np.float32).astype(ml_dtypes.bfloat16)
    return high, low


def split(value):
    high = value.astype(BF16)
    return high, (value - high.astype(F32)).astype(BF16)


def mul(left, right, dims):
    return lax.dot_general(left, right, dims, preferred_element_type=F32)


def triple(left, high, low, dims):
    first, second = split(left)
    return mul(first, high, dims) + mul(first, low, dims) + mul(second, high, dims)


def inverted(value):
    guess = pl.reciprocal(value, approx=True)
    guess = guess * (2.0 - value * guess)
    return guess * (2.0 - value * guess)


def exact(left, right, dims):
    return lax.dot_general(left, right, dims, precision=EXACT, preferred_element_type=F32)


def solid_values(x, y, z):
    squared = x * x + y * y + z * z
    cosine, sine = {}, {}
    cosine[0, 0], sine[0, 0] = np.ones_like(x), np.zeros_like(x)
    for l in range(1, COUNT):
        scale = math.sqrt((2 * l - 1) / (2.0 * l)) if l > 1 else 1.0
        cosine[l, l] = scale * (x * cosine[l - 1, l - 1] - y * sine[l - 1, l - 1])
        sine[l, l] = scale * (x * sine[l - 1, l - 1] + y * cosine[l - 1, l - 1])
    for table in (cosine, sine):
        for m in range(COUNT):
            for l in range(m + 1, COUNT):
                older = table[l - 2, m] if l - 2 >= m else np.zeros_like(x)
                table[l, m] = (
                    (2 * l - 1) * z * table[l - 1, m]
                    - math.sqrt((l - 1) ** 2 - m * m) * squared * older
                ) / math.sqrt(l * l - m * m)
    return [(cosine, sine)[kind][l, m] for kind, l, m in term_list()]


@functools.cache
def constants(length):
    step = length + 1
    index = np.arange(length) + 1
    sine = np.sin(np.pi * ((index[:, None] * index[None, :]) % (2 * step)) / step)
    eigen = 4.0 * np.sin(np.pi * index / (2.0 * step)) ** 2
    cells = (np.arange(length) - (length - 1) / 2.0) / step
    legendre = np.stack(
        [np.polynomial.legendre.legval(2 * cells, np.eye(COUNT)[p]) for p in range(COUNT)]
    )
    hat = legendre @ sine
    edges = np.stack([sine[0] + sine[-1], sine[-1] - sine[0]])
    lookup = np.concatenate([hat, edges])
    columns = np.zeros((length, 128))
    columns[:, : COUNT + 2] = lookup.T
    spread = np.zeros((2, 128, PAIRS))
    own = np.zeros((2, 24, PAIRS))
    for spot, pair in enumerate(pair_list()):
        for kind in range(2):
            spread[kind, pair[kind], spot] = 1.0
            own[kind, pair[kind], spot] = 1.0
    nodes, weights = np.polynomial.legendre.leggauss(COUNT + 3)
    basis = np.stack([np.polynomial.legendre.legval(nodes, np.eye(COUNT)[p]) for p in range(COUNT)])
    project = basis * weights[None, :] * (2 * np.arange(COUNT)[:, None] + 1) / 2.0
    first, second = np.meshgrid(nodes / 2.0, nodes / 2.0, indexing="ij")
    half = np.full_like(first, 0.5)
    terms = term_list()
    scale = (1.0 / step) * (2.0 / step) ** 2
    maps = np.zeros((3, PAIRS, TERMS))
    places = [(half, first, second), (first, half, second), (first, second, half)]
    for face, place in enumerate(places):
        for column, values in enumerate(solid_values(*place)):
            degree = terms[column][1]
            expansion = project @ values @ project.T
            for spot, pair in enumerate(pair_list()):
                maps[face, spot, column] = scale * expansion[pair] / radius_scale**degree
    masks = np.zeros((3, 8, TERMS))
    for column, (kind, l, m) in enumerate(terms):
        masks[0, (m + kind) % 2, column] = 1.0
        masks[1, kind, column] = 1.0
        masks[2, (l - m) % 2, column] = 1.0
    folded = np.zeros((2, length // 2, length))
    parity = np.arange(length) % 2
    upper = 2.0 * sine[length // 2 :]
    folded[0] = upper * (parity == 0)
    folded[1] = upper * (parity == 1)
    return dict(
        sine=sine,
        eigen=eigen,
        cells=cells,
        legendre=legendre,
        columns=columns,
        spread=spread,
        own=own,
        edges=edges,
        maps=maps,
        masks=masks,
        folded=folded.reshape(length, length),
    )


def evaluation_scales():
    sector, running = [1.0], 1.0
    for l in range(1, COUNT):
        running *= math.sqrt((2 * l - 1) / (2.0 * l)) if l > 1 else 1.0
        sector.append(running)
    kappa, beta = {}, {}
    for m in range(COUNT):
        kappa[m, m] = sector[m]
        previous = 1.0
        for l in range(m + 1, COUNT):
            near = (2 * l - 1) / math.sqrt(l * l - m * m)
            far = math.sqrt((l - 1) ** 2 - m * m) / math.sqrt(l * l - m * m)
            kappa[l, m] = kappa[l - 1, m] * near
            beta[l, m] = far / (near * previous) if l >= m + 2 else 0.0
            previous = near
    scales = np.zeros((8, TERMS))
    for row, (_, l, m) in enumerate(term_list()):
        factor = 1.0 if m == 0 else 2.0
        weight = factor / (4.0 * math.pi * radius_scale * outer_ratio ** (l + 1))
        scales[:, row] = weight * kappa[l, m]
    return scales, beta


def evaluate(coef, unit_x, unit_y, unit_z):
    beta = evaluation_scales()[1]
    rows = {term: row for row, term in enumerate(term_list())}
    total = {}

    def add(key, value):
        total[key] = value if key not in total else total[key] + value

    cosine, sine = None, None
    for m in range(COUNT):
        if m == 1:
            cosine, sine = unit_x, unit_y
        elif m > 1:
            cosine, sine = unit_x * cosine - unit_y * sine, unit_x * sine + unit_y * cosine
        sums = {}
        older, newer = None, None
        for l in range(m, COUNT):
            if l == m:
                now = None
            elif l == m + 1:
                now = unit_z
            elif l == m + 2:
                now = unit_z * newer - beta[l, m]
            else:
                now = unit_z * newer - beta[l, m] * older
            for kind in range(1 if m == 0 else 2):
                row = rows[kind, l, m]
                weight = coef[row : row + 1, :]
                weight = jnp.broadcast_to(weight, unit_z.shape)
                term = weight if now is None else weight * now
                key = (kind, (l - m) % 2)
                sums[key] = term if key not in sums else sums[key] + term
            older, newer = newer, now
        for (kind, odd), value in sums.items():
            if m > 0:
                value = value * (cosine, sine)[kind]
            add((m % 2, kind, odd), value)
    return total


RESIDENT = pl.BlockSpec(memory_space=pltpu.VMEM)
SCALARS = pl.BlockSpec(memory_space=pltpu.SMEM)


def call(body, grid, in_specs, out_specs, out_shape, scratch, flops, aliases=None, limit=24):
    kernel = pl.pallas_call(
        body,
        grid=grid,
        in_specs=in_specs,
        out_specs=out_specs,
        out_shape=out_shape,
        scratch_shapes=scratch,
        input_output_aliases=aliases or {},
        cost_estimate=pl.CostEstimate(flops=flops, bytes_accessed=4 << 20, transcendentals=0),
        compiler_params=pltpu.CompilerParams(
            dimension_semantics=("arbitrary",) * len(grid), vmem_limit_bytes=limit << 20
        ),
    )

    def run(*args):
        placed = []
        for arg, spec in zip(args, in_specs):
            if spec is RESIDENT:
                arg = pltpu.with_memory_space_constraint(arg, pltpu.VMEM)
            elif spec.block_shape is not None:
                arg = pltpu.with_memory_space_constraint(arg, pltpu.HBM)
            placed.append(arg)
        return kernel(*placed)

    return run


def kept(*shape):
    return pltpu.VMEM(shape, F32)


def shards(charge_density):
    cells_a, cells_b, length = charge_density.shape
    groups_x, groups_y = lax.axis_size("gx"), lax.axis_size("gy")
    devices = groups_x * groups_y
    index_x, index_y = lax.axis_index("gx"), lax.axis_index("gy")
    tabs = constants(length)
    spacing = 1.0 / (length + 1)
    pack = max(1, 128 // cells_b)
    lanes = pack * cells_b
    wide = pack * length
    tiles = cells_a // pack
    depth = cells_b
    block = min(64, depth)
    blocks = depth // block
    modes = depth // groups_x
    ghosts = 2 * groups_x
    functions = COUNT + 2
    place = jnp.stack([index_x, index_y]).astype(jnp.int32)

    def const(name):
        return jnp.asarray(tabs[name].astype(np.float32))

    sine_high, sine_low = (jnp.asarray(t) for t in split_np(tabs["sine"]))
    sine_high = sine_high.reshape(groups_y, cells_b, length)
    sine_low = sine_low.reshape(groups_y, cells_b, length)
    parts_in = tiles // 4 if tiles % 4 == 0 else tiles
    uneven = parts_in < tiles
    going = [parts_in, 3 * parts_in] if uneven else [tiles]
    coming = [parts_in, 2 * parts_in, parts_in] if uneven else [tiles]

    def starts_of(portions):
        return [sum(portions[:number]) for number in range(len(portions))]

    pair_limit = 24 if wide <= 512 else 44

    def fill_pairs(weights, high_ref, low_ref, index_y):
        weights[...] = jnp.zeros_like(weights)
        for shift in range(groups_y):
            peer = index_y ^ shift
            for item in range(pack):
                rows = pl.ds(shift * lanes + item * cells_b, cells_b)
                weights[0, rows, item * length : (item + 1) * length] = high_ref[peer]
                weights[1, rows, item * length : (item + 1) * length] = low_ref[peer]

    many = min(4, parts_in)

    def depth_body(place_ref, rho_ref, high_ref, low_ref, *rest):
        outs, table = rest[:groups_y], rest[groups_y]

        @pl.when(pl.program_id(0) == 0)
        def _():
            for shift in range(groups_y):
                peer = place_ref[1] ^ shift
                table[0, pl.ds(shift * cells_b, cells_b), :] = high_ref[peer]
                table[1, pl.ds(shift * cells_b, cells_b), :] = low_ref[peer]

        value = rho_ref[...].reshape(many * lanes, length)
        high, low = split(value)
        result = mul(table[0], high, NT) + mul(table[1], high, NT) + mul(table[0], low, NT)
        start = pl.program_id(0) * many
        for shift in range(groups_y):
            for item in range(many):
                outs[shift][start + item] = result[
                    shift * cells_b : (shift + 1) * cells_b, item * lanes : (item + 1) * lanes
                ]

    def pieces_of(count):
        return [kept(count, depth, lanes)] * groups_y

    table_spec = pl.BlockSpec((groups_y, cells_b, length), lambda t: (0, 0, 0))

    def depth_transform(number):
        steps, first = going[number] // many, starts_of(going)[number] // many
        return call(
            depth_body,
            (steps,),
            [
                SCALARS,
                pl.BlockSpec((many * pack, cells_b, length), lambda t: (t + first, 0, 0)),
                table_spec,
                table_spec,
            ],
            [RESIDENT] * groups_y,
            pieces_of(going[number]),
            [pltpu.VMEM((2, length, length), BF16)],
            10**9,
        )(
            place,
            charge_density,
            sine_high,
            sine_low,
        )

    def exchange(parts):
        received = [parts[0]]
        for shift in range(1, groups_y):
            ring = [(source, source ^ shift) for source in range(groups_y)]
            received.append(lax.ppermute(parts[shift], "gy", ring))
        return received

    received = []
    for number in range(len(going)):
        parts = depth_transform(number)
        received.append(exchange(parts))

    half = length // 2
    sine64 = tabs["sine"]
    scale = 2.0 / (length + 1)
    hat_all = scale * np.concatenate([tabs["legendre"] @ sine64, tabs["edges"]])
    hat_pad = -(-functions // 8) * 8
    hat_all = np.concatenate([hat_all, np.zeros((hat_pad - functions, length))])
    blank = np.zeros((1, length))
    lines = np.concatenate([blank, sine64, blank])
    spots = []
    for slab in range(groups_x):
        spots += [slab * cells_a, (slab + 1) * cells_a + 1]
    green_lines = lines[spots]
    green = (scale * green_lines[:, None, :] * green_lines[None, :, :]).reshape(-1, length)
    eigen_column = np.broadcast_to(tabs["eigen"][:, None], (length, length))
    eigen_row = np.broadcast_to(tabs["eigen"][None, :], (8, length))
    cell_column = np.broadcast_to(tabs["cells"][:, None], (length, half))
    cell_row = np.broadcast_to(tabs["cells"][None, half:], (8, half))

    def put(table):
        return jnp.asarray(np.ascontiguousarray(table).astype(np.float32))

    def prepare_body(
        place_ref,
        column_ref,
        row_ref,
        line_ref,
        hat_ref,
        green_high_ref,
        green_low_ref,
        cell_column_ref,
        cell_row_ref,
        sine_high_ref,
        sine_low_ref,
        factor_ref,
        profile_ref,
        probe_ref,
        green_ref,
        unit_ref,
        pair_ref,
        table_ref,
        values,
        probe_high,
        probe_low,
    ):
        index_x, index_y = place_ref[0], place_ref[1]
        fill_pairs(pair_ref, sine_high_ref, sine_low_ref, index_y)
        for shift in range(groups_y):
            peer = index_y ^ shift
            table_ref[0, pl.ds(shift * cells_b, cells_b), :] = sine_high_ref[peer]
            table_ref[1, pl.ds(shift * cells_b, cells_b), :] = sine_low_ref[peer]
        own = pl.ds(pl.multiple_of(index_y * depth, depth), depth)
        values[...] = column_ref[own, :] + row_ref[0:1, :]
        value = values[...] + 2.0
        factor = inverted(value)
        running = factor
        factor_ref[0] = factor
        profile_ref[0] = running
        for row in range(1, cells_a):
            factor = inverted(value - factor)
            running = running * factor
            factor_ref[row] = factor
            profile_ref[row] = running
        for row in range(cells_a - 2, -1, -1):
            running = profile_ref[row] + factor_ref[row] * running
            profile_ref[row] = running
        for side in range(2):
            spot = index_x * cells_a + side * (cells_a + 1)
            table = line_ref[pl.ds(spot, 1), :] * hat_ref[...]
            high, low = split(table)
            probe_high[side * hat_pad : (side + 1) * hat_pad] = high
            probe_low[side * hat_pad : (side + 1) * hat_pad] = low

        def inverse_of(spot):
            return split(inverted(column_ref[...] + values[pl.ds(spot, 1), :]))

        def probe_step(number, carry):
            high, low = inverse_of(number)
            answer = (
                mul(probe_high[...], high, NN)
                + mul(probe_low[...], high, NN)
                + mul(probe_high[...], low, NN)
            )
            rows = pl.ds(pl.multiple_of(number * 2 * hat_pad, 8), 2 * hat_pad)
            for part in range(length // 128):
                probe_ref[part, rows, :] = answer[:, part * 128 : (part + 1) * 128]
            return carry

        lax.fori_loop(0, depth, probe_step, 0, unroll=4)

        def green_step(number, carry):
            high, low = inverse_of(index_x * modes + number)
            answer = (
                mul(green_high_ref[...], high, NN)
                + mul(green_low_ref[...], high, NN)
                + mul(green_high_ref[...], low, NN)
            )
            green_ref[pl.ds(number, 1)] = answer[None]
            return carry

        lax.fori_loop(0, modes, green_step, 0, unroll=min(2, modes))
        here = pl.ds(pl.multiple_of(index_x * cells_a, cells_a), cells_a)
        middle = jnp.full((8, half), 0.5, F32)[0:1]
        along = cell_row_ref[0:1, :]
        for begin, count, first, second, third in (
            (0, cells_a, cell_column_ref[here, :], middle, along),
            (cells_a, cells_a, cell_column_ref[here, :], along, middle),
            (2 * cells_a, half, middle, cell_column_ref[half:, :], along),
        ):
            inverse = 1.0 / jnp.sqrt(first * first + second * second + third * third)
            unit_ref[0, begin : begin + count] = first * inverse
            unit_ref[1, begin : begin + count] = second * inverse
            unit_ref[2, begin : begin + count] = third * inverse

    field = kept(cells_a, depth, length)
    green_high, green_low = (jnp.asarray(t) for t in split_np(green))
    inputs = (
        put(eigen_column),
        put(eigen_row),
        put(lines),
        put(hat_all),
        green_high,
        green_low,
        put(cell_column),
        put(cell_row),
        sine_high,
        sine_low,
    )

    def block_of(array):
        zeros = (0,) * array.ndim
        return pl.BlockSpec(array.shape, lambda k: zeros)

    tables = call(
        prepare_body,
        (1,),
        [SCALARS] + [block_of(array) for array in inputs],
        [RESIDENT] * 7,
        [
            field,
            field,
            kept(length // 128, depth * 2 * hat_pad, 128),
            kept(modes, ghosts * ghosts, length),
            kept(3, 2 * cells_a + half, half),
            pltpu.VMEM((2, groups_y * lanes, wide), BF16),
            pltpu.VMEM((2, length, length), BF16),
        ],
        [
            pltpu.VMEM((depth, length), F32),
            pltpu.VMEM((2 * hat_pad, length), BF16),
            pltpu.VMEM((2 * hat_pad, length), BF16),
        ],
        10**10,
        limit=pair_limit,
    )(place, *inputs)
    legendre = put(tabs["legendre"])
    edge_rows = put(np.concatenate([tabs["edges"], np.zeros((6, length))]))
    edge_columns = put(np.broadcast_to(tabs["edges"][:, :, None], (2, length, 128)))
    column_high, column_low = (jnp.asarray(t) for t in split_np(tabs["columns"]))
    lookup = np.zeros((groups_y, 24, depth))
    lookup[:, : COUNT + 2] = (
        tabs["columns"][:, : COUNT + 2].T.reshape(COUNT + 2, groups_y, depth).transpose(1, 0, 2)
    )
    lookup = lookup.reshape(groups_y, 24, blocks, block).transpose(0, 2, 1, 3)
    lookup_high, lookup_low = (jnp.asarray(t) for t in split_np(lookup))
    spread = jnp.asarray(tabs["spread"].astype(np.float32)).astype(BF16)
    map_high, map_low = (jnp.asarray(t) for t in split_np(tabs["maps"]))
    factors, profile, probe_table, green_table, units, pairs, table = tables

    def second_body(*refs):
        blocks_in = refs[:groups_y]
        weights, out_ref = refs[groups_y:]
        part_tiles = out_ref.shape[0] // pack
        for start in range(0, depth, block):
            value = jnp.concatenate(
                [
                    part[:, start : start + block, :].reshape(part_tiles * block, lanes)
                    for part in blocks_in
                ],
                axis=1,
            )
            result = triple(value, weights[0], weights[1], NN) * (spacing * spacing)
            for item in range(part_tiles):
                for inner in range(pack):
                    out_ref[item * pack + inner, start : start + block, :] = result[
                        item * block : (item + 1) * block, inner * length : (inner + 1) * length
                    ]

    sources = []
    for number, parts in enumerate(received):
        sources.append(
            call(
                second_body,
                (1,),
                [RESIDENT] * (groups_y + 1),
                RESIDENT,
                kept(going[number] * pack, depth, length),
                [],
                10**9,
                limit=pair_limit,
            )(*parts, pairs)
        )

    rows_now = min(32, block)

    def solve_body(place_ref, leg_ref, *refs):
        given = refs[: len(going)]
        (
            factor_ref,
            probe_ref,
            column_high_ref,
            column_low_ref,
            lookup_high_ref,
            lookup_low_ref,
            spread_ref,
            own_ref,
            map_high_ref,
            map_low_ref,
            mask_ref,
            field_ref,
            moment_ref,
            energy_ref,
            tensor,
        ) = refs[len(going) :]
        index_x, index_y = place_ref[0], place_ref[1]
        begin = jnp.where(index_x == 0, 1.0, 0.0)
        finish = jnp.where(index_x == groups_x - 1, 1.0, 0.0)
        step = pl.program_id(0)
        base = pl.multiple_of(step * block, block)
        window = pl.ds(base, block)

        @pl.when(step == 0)
        def _():
            tensor[...] = jnp.zeros_like(tensor)
            energy_ref[...] = jnp.zeros_like(energy_ref)

        def source(row, begin_row):
            starts = starts_of(going)
            number = max(n for n in range(len(going)) if starts[n] * pack <= row)
            return given[number][row - starts[number] * pack, pl.ds(begin_row, rows_now), :]

        def eliminate(begin_row):
            strip = pl.ds(begin_row, rows_now)
            running = source(0, begin_row) * factor_ref[0, strip, :]
            field_ref[0, strip, :] = running
            for row in range(1, cells_a):
                running = (source(row, begin_row) + running) * factor_ref[row, strip, :]
                field_ref[row, strip, :] = running
            energy = source(cells_a - 1, begin_row) * running
            for row in range(cells_a - 2, -1, -1):
                running = field_ref[row, strip, :] + factor_ref[row, strip, :] * running
                field_ref[row, strip, :] = running
                energy = energy + source(row, begin_row) * running
            energy = jnp.sum(energy.reshape(rows_now // 8, 8, length), axis=0)
            for part in range(length // 128):
                energy_ref[...] += energy[:, part * 128 : (part + 1) * 128]

        for offset in range(0, block, rows_now):
            eliminate(pl.multiple_of(base + offset, rows_now))
        first, last = field_ref[0, window, :], field_ref[cells_a - 1, window, :]
        table_high, table_low = column_high_ref[...], column_low_ref[...]
        rows_high = lookup_high_ref[index_y, step]
        rows_low = lookup_low_ref[index_y, step]

        def contract(stack, count):
            answer = triple(stack, table_high, table_low, NN)
            upper, lower = split(answer)
            outs = []
            for item in range(count):
                high = upper[item * block : (item + 1) * block]
                low = lower[item * block : (item + 1) * block]
                outs.append(
                    mul(rows_high, high, NN) + mul(rows_low, high, NN) + mul(rows_high, low, NN)
                )
            return outs

        many_rows = min(16, cells_a)
        for start in range(0, cells_a, many_rows):
            stack = field_ref[start : start + many_rows, window, :].reshape(
                many_rows * block, length
            )
            outs = contract(stack, many_rows)
            for item in range(COUNT):
                value = tensor[item]
                for inner, out in enumerate(outs):
                    value = value + leg_ref[item, index_x * cells_a + start + inner] * out
                tensor[item] = value
            if start == 0:
                tensor[COUNT] += begin * outs[0]
                tensor[COUNT + 1] -= begin * outs[0]
            if start + many_rows == cells_a:
                tensor[COUNT] += finish * outs[-1]
                tensor[COUNT + 1] += finish * outs[-1]

        def probe_row(item):
            rows = pl.ds(base * 2 * hat_pad + item, block, stride=2 * hat_pad)
            return jnp.concatenate(
                [probe_ref[part, rows, :] for part in range(length // 128)], axis=1
            )

        group = 10
        for start in range(0, functions, group):
            items = range(start, min(start + group, functions))
            stack = jnp.concatenate(
                [
                    probe_row(item) * first + probe_row(hat_pad + item) * last
                    for item in items
                ],
                axis=0,
            )
            for item, out in zip(items, contract(stack, len(items))):
                tensor[item] += out

        @pl.when(step == blocks - 1)
        def _():
            rows = lax.broadcasted_iota(jnp.int32, (8, PAIRS), 0)

            def flatten(matrix, kind):
                high, low = split(matrix)
                answer = mul(high, spread_ref[kind], NN) + mul(low, spread_ref[kind], NN)
                return jnp.sum(answer * own_ref[1 - kind], axis=0, keepdims=True)

            moments = jnp.zeros((8, TERMS), F32)
            for face in range(3):
                stack = jnp.zeros((8, PAIRS), F32)
                for parity in range(2):
                    if face == 0:
                        value = flatten(tensor[COUNT + parity], 0)
                    elif face == 1:
                        value = jnp.zeros((1, PAIRS), F32)
                        for item in range(COUNT):
                            column = tensor[item, :, COUNT + parity : COUNT + parity + 1]
                            chosen = own_ref[0, item : item + 1, :] * own_ref[1]
                            value = value + jnp.sum(column * chosen, axis=0, keepdims=True)
                    else:
                        matrix = jnp.concatenate(
                            [
                                tensor[item, COUNT + parity : COUNT + parity + 1, :]
                                for item in range(COUNT)
                            ]
                            + [jnp.zeros((24 - COUNT, 128), F32)],
                            axis=0,
                        )
                        high, low = split(matrix)
                        answer = mul(high, spread_ref[1], NN) + mul(low, spread_ref[1], NN)
                        value = jnp.sum(answer * own_ref[0], axis=0, keepdims=True)
                    stack = jnp.where(rows == parity, value, stack)
                moments = moments + triple(stack, map_high_ref[face], map_low_ref[face], NN) * (
                    mask_ref[face]
                )
            moments = jnp.sum(moments, axis=0, keepdims=True)
            moment_ref[...] = jnp.broadcast_to(moments[None], moment_ref.shape)

    solved, moments, energy_one = call(
        solve_body,
        (blocks,),
        [SCALARS] * 2 + [RESIDENT] * (len(going) + 11),
        [RESIDENT] * 3,
        [field, kept(devices, 1, TERMS), kept(8, 128)],
        [
            pltpu.VMEM((24, 24, 128), F32),
        ],
        10**9,
    )(
        place,
        legendre,
        *sources,
        factors,
        probe_table,
        column_high,
        column_low,
        lookup_high,
        lookup_low,
        spread,
        const("own"),
        map_high,
        map_low,
        const("masks"),
    )
    shared = lax.all_to_all(moments, ("gx", "gy"), 0, 0, tiled=True)

    scales = jnp.asarray(evaluation_scales()[0].astype(np.float32))
    folded_high, folded_low = (jnp.asarray(t) for t in split_np(tabs["folded"]))
    local_high, local_low = (
        jnp.asarray(np.ascontiguousarray(t.T).reshape(groups_y, depth, length))
        for t in split_np(tabs["folded"])
    )
    strip = min(32, cells_a)
    shares_count = block // modes
    face_rows = min(FACE_ROWS, block)

    def source_body(
        place_ref,
        share_ref,
        scale_ref,
        unit_ref,
        folded_high_ref,
        folded_low_ref,
        local_high_ref,
        local_low_ref,
        row_ref,
        column_ref,
        factor_ref,
        solved_ref,
        total_ref,
        near_ref,
        energy_ref,
        coef,
        values,
        plane_x,
        plane_y,
        plane_z,
        lines_y,
        lines_z,
        walls,
    ):
        index_x, index_y = place_ref[0], place_ref[1]
        begin = jnp.where(index_x == 0, 1.0, 0.0)
        finish = jnp.where(index_x == groups_x - 1, 1.0, 0.0)

        step = pl.program_id(0)
        window = pl.ds(pl.multiple_of(step * block, block), block)

        @pl.when(step == 0)
        def _():
            ones = jnp.full((8, 128), 0.125, F32)
            shares = jnp.sum(share_ref[...], axis=0) * scale_ref[...]
            coef[...] = exact(shares, ones, TN)
            energy_ref[...] = jnp.zeros_like(energy_ref)

            def one_strip(number, carry):
                window = pl.ds(pl.multiple_of(number * strip, strip), strip)
                classes = evaluate(
                    coef, unit_ref[0, window, :], unit_ref[1, window, :], unit_ref[2, window, :]
                )
                for (azimuth, kind, odd), value in classes.items():
                    values[azimuth * 4 + kind * 2 + odd, window, :] = value
                return carry

            lax.fori_loop(0, (2 * cells_a + half) // strip, one_strip, 0)
            for kind in range(2):
                for odd in range(2):
                    for start, target, row, column in (
                        (0, plane_y, kind, odd),
                        (cells_a, plane_z, odd, kind),
                    ):
                        target[
                            row * cells_a : (row + 1) * cells_a, column * half : (column + 1) * half
                        ] = (
                            values[kind * 2 + odd, start : start + cells_a, :]
                            + values[4 + kind * 2 + odd, start : start + cells_a, :]
                        )
                    even, other = (
                        values[parity * 4 + kind * 2 + odd, 2 * cells_a :, :]
                        for parity in (kind, 1 - kind)
                    )
                    plane_x[
                        kind * half : (kind + 1) * half, odd * half : (odd + 1) * half
                    ] = even + (finish - begin) * other
            folded_tables = folded_high_ref[...], folded_low_ref[...]
            local_tables = local_high_ref[index_y], local_low_ref[index_y]

            def across(plane):
                upper, lower = split(plane)
                high, low = local_tables
                return mul(high, upper, NT) + mul(low, upper, NT) + mul(high, lower, NT)

            lines_z[...] = triple(plane_z[...], *folded_tables, NN)
            lines_y[...] = across(plane_y[...])
            wall = triple(across(plane_x[...]), *folded_tables, NN)
            walls[0] = begin * wall
            walls[1] = finish * wall


        def eliminate(offset):
            begin_row = pl.multiple_of(step * block + offset, face_rows)
            window = pl.ds(begin_row, face_rows)
            here = pl.ds(pl.multiple_of(index_y * depth + begin_row, face_rows), face_rows)
            columns = [
                jnp.concatenate([column_ref[parity, here, :]] * (length // 128), axis=1)
                for parity in range(2)
            ]
            line_block = lines_y[window, :]
            energy = jnp.zeros((face_rows, length), F32)
            running = None
            for row in range(cells_a):
                value = None
                for parity in range(2):
                    spot = parity * cells_a + row
                    term = line_block[:, spot : spot + 1] * row_ref[parity : parity + 1, :]
                    value = term if value is None else value + term
                    value = value + lines_z[spot : spot + 1, :] * columns[parity]
                if row == 0:
                    value = value + walls[0, window, :]
                if row == cells_a - 1:
                    value = value + walls[1, window, :]
                energy = energy + value * solved_ref[row, window, :]
                running = value if running is None else value + running
                running = running * factor_ref[row, window, :]
                total_ref[row, window, :] = running
            nears = [solved_ref[0, window, :], solved_ref[cells_a - 1, window, :], None, running]
            total_ref[cells_a - 1, window, :] = nears[1] + running
            for row in range(cells_a - 2, -1, -1):
                running = total_ref[row, window, :] + factor_ref[row, window, :] * running
                total_ref[row, window, :] = solved_ref[row, window, :] + running
            nears[2] = running
            for item in range(face_rows // modes):
                for number, value in enumerate(nears):
                    near_ref[(step * block + offset) // modes + item, number] = value[
                        item * modes : (item + 1) * modes
                    ]
            energy = jnp.sum(energy.reshape(face_rows // 8, 8, length), axis=0)
            for part in range(length // 128):
                energy_ref[...] += energy[:, part * 128 : (part + 1) * 128]

        for offset in range(0, block, face_rows):
            eliminate(offset)

    total, nears, energy_two = call(
        source_body,
        (blocks,),
        [SCALARS] + [RESIDENT] * 11,
        [RESIDENT] * 3,
        [field, kept(groups_x, 4, modes, length), kept(8, 128)],
        [
            pltpu.VMEM((TERMS, 128), F32),
            kept(8, 2 * cells_a + half, half),
            pltpu.VMEM((length, length), F32),
            pltpu.VMEM((2 * cells_a, length), F32),
            pltpu.VMEM((2 * cells_a, length), F32),
            pltpu.VMEM((depth, 2 * cells_a), F32),
            pltpu.VMEM((2 * cells_a, length), F32),
            pltpu.VMEM((2, depth, length), F32),
        ],
        10**9,
    )(
        place,
        shared,
        scales,
        units,
        folded_high,
        folded_low,
        local_high,
        local_low,
        edge_rows,
        edge_columns,
        factors,
        solved,
    )

    gathered = lax.all_to_all(nears, "gx", 0, 0, tiled=True)

    def ghost_body(near_ref, green_ref, one_ref, two_ref, out_ref):
        first = [near_ref[s, 0] for s in range(groups_x)]
        last = [near_ref[s, 1] for s in range(groups_x)]
        other_first = [near_ref[s, 2] for s in range(groups_x)]
        other_last = [near_ref[s, 3] for s in range(groups_x)]
        energy_one = jnp.zeros((modes, length), F32)
        energy_two = jnp.zeros((modes, length), F32)
        for slab in range(groups_x):
            for side in range(2):
                value = jnp.zeros((modes, length), F32)
                other = jnp.zeros((modes, length), F32)
                neighbour = slab + (1 if side else -1)
                if 0 <= neighbour < groups_x:
                    value = (first if side else last)[neighbour]
                    other = (other_first if side else other_last)[neighbour]
                    base = (2 * slab + side) * ghosts
                    for s in range(groups_x):
                        near, far = green_ref[:, base + 2 * s, :], green_ref[:, base + 2 * s + 1, :]
                        value = value + near * first[s] + far * last[s]
                        other = other + near * other_first[s] + far * other_last[s]
                energy_one = energy_one + value * (last if side else first)[slab]
                energy_two = energy_two + value * (other_last if side else other_first)[slab]
                out_ref[slab, side * modes : (side + 1) * modes, :] = value + other
        top = lax.broadcasted_iota(jnp.int32, (8, 128), 0) == 0
        for number, (local_ref, value) in enumerate(((one_ref, energy_one), (two_ref, energy_two))):
            value = jnp.sum(value, axis=0, keepdims=True)
            line = value[:, 0:128]
            for part in range(1, length // 128):
                line = line + value[:, part * 128 : (part + 1) * 128]
            tile = local_ref[...] + jnp.where(top, line, 0.0)
            for slab in range(groups_x):
                out_ref[slab, 2 * modes : 2 * modes + 8, number * 128 : (number + 1) * 128] = tile

    height = 2 * modes + 8
    answers = call(
        ghost_body, (1,), [RESIDENT] * 4, RESIDENT, kept(groups_x, height, length), [], 10**8
    )(gathered, green_table, energy_one, energy_two)
    returned = lax.all_to_all(answers, "gx", 0, 0, tiled=True)

    def back_body(number, total_ref, profile_ref, ghost_ref, weights, *rest):
        outs, energy_ref = rest[:groups_y], rest[groups_y]
        energy_ref[...] = jnp.sum(ghost_ref[:, 2 * modes : 2 * modes + 8, 0:256], axis=0)
        for step in range(blocks):
            back_block(total_ref, profile_ref, ghost_ref, outs, weights, step, number)

    def back_block(total_ref, profile_ref, ghost_ref, outs, weights, step, number):
        window = pl.ds(step * block, block)
        ghosts_here = [
            jnp.concatenate(
                [
                    ghost_ref[step * shares_count + item, side * modes : (side + 1) * modes, :]
                    for item in range(shares_count)
                ],
                axis=0,
            )
            for side in range(2)
        ]

        parts = []
        for item in range(starts_of(coming)[number], starts_of(coming)[number] + coming[number]):
            inner = []
            for row in range(item * pack, (item + 1) * pack):
                inner.append(
                    total_ref[row, window, :]
                    + profile_ref[row, window, :] * ghosts_here[0]
                    + profile_ref[cells_a - 1 - row, window, :] * ghosts_here[1]
                )
            parts.append(jnp.concatenate(inner, axis=1))
        result = triple(jnp.concatenate(parts, axis=0), weights[0], weights[1], NT)
        for shift in range(groups_y):
            for item in range(coming[number]):
                outs[shift][item, window, :] = result[
                    item * block : (item + 1) * block, shift * lanes : (shift + 1) * lanes
                ]

    arrived = []
    for number in range(len(coming)):
        *parts, tile_now = call(
            functools.partial(back_body, number),
            (1,),
            [RESIDENT] * 4,
            [RESIDENT] * (groups_y + 1),
            pieces_of(coming[number]) + [kept(8, 256)],
            [],
            10**9,
            limit=pair_limit,
        )(total, profile, returned, pairs)
        energy_tile = tile_now if number == 0 else energy_tile
        arrived.append(exchange(parts))
    energy_tiles = exchange([energy_tile] * groups_y)

    norm = (2.0 / (length + 1)) ** 2

    def last_body(*refs):
        blocks_in = refs[:groups_y]
        table, out_ref = refs[groups_y], refs[-1]
        start = pl.program_id(0) * many
        values = [
            jnp.concatenate([part[start + item] for part in blocks_in], axis=0).T
            for item in range(many)
        ]
        result = triple(jnp.concatenate(values, axis=0), table[0], table[1], NN) * norm
        out_ref[...] = result.reshape(many * pack, cells_b, length)

    def final_body(*refs):
        tiles_in = refs[-2 - groups_y : -2]
        energy_ref = refs[-1]
        last_body(*refs[: groups_y + 1], refs[-2])

        @pl.when(pl.program_id(0) == 0)
        def _():
            value = tiles_in[0][...]
            for tile in tiles_in[1:]:
                value = value + tile[...]
            factor = spacing * norm
            first = jnp.sum(value[:, 0:128]) * factor
            energy_ref[0] = first
            energy_ref[1] = first + jnp.sum(value[:, 128:256]) * factor

    shape = jax.ShapeDtypeStruct(charge_density.shape, F32)
    base_specs = [RESIDENT] * (groups_y + 1)
    out_block = (many * pack, cells_b, length)
    potential = None
    for number in range(len(coming)):
        steps, first = coming[number] // many, starts_of(coming)[number] // many
        inputs = [*arrived[number], table]
        specs, aliases = list(base_specs), None
        if number > 0:
            aliases = {len(inputs): 0}
            inputs.append(potential)
            specs.append(pl.BlockSpec(memory_space=pl.ANY))
        out_spec = pl.BlockSpec(out_block, lambda t, first=first: (t + first, 0, 0))
        if number < len(coming) - 1:
            potential = call(
                last_body, (steps,), specs, out_spec, shape, [], 10**9, aliases
            )(*inputs)
        else:
            potential, energies = call(
                final_body,
                (steps,),
                specs + [RESIDENT] * groups_y,
                [out_spec, SCALARS],
                [shape, jax.ShapeDtypeStruct((2,), F32)],
                [],
                10**9,
                aliases,
            )(*inputs, *energy_tiles)
    return potential, energies


def solution(mesh):
    placed = (P("gx", "gy", None),)
    return jax.shard_map(
        shards, mesh=mesh, in_specs=placed, out_specs=(P("gx", "gy", None), P()), check_vma=False
    )
```

profile of v0, /device:TPU:0, one launch (start us, length us, event | category | flops | bytes accessed | tf_op | source)
XLA Modules:
  0.0 115.4 jit_solution(15845785580373739809)
XLA Ops:
  0.7 1.5 %shard_map.275 = (f32[4,64,128]{2,1,0:T(8,128)S(1)}, f32[4,64,128]{2,1,0:T(8,128)S(1)}, f32[4,64,128]{2,1,0:T(8,128)S(1)}, f32[4,64,128]{2,1,0:T(8,128)S(1)}) custom-call(s32[2]{0:T(128)S(1)} %pad_add_fusion.place_ref, f32[32,64,256]{2,1,0:T(8,128)} %rho_ref.3, bf16[4,64,256]{2,1,0:T(8,128)(2,1)} %constant.90.high_ref.sine_high_ref, ...), custom_call_target="tpu_custom_call" | custom-call | flops 1000000000 | bytes 4194304 | tf_op jit(solution)/shard_map/pallas_call | solution.py:241
  2.2 0.6 collective-permute-start
  2.8 2.6 %collective-permute-start.1 = (f32[4,64,128]{2,1,0:T(8,128)S(1)}, f32[4,64,128]{2,1,0:T(8,128)S(1)}, u32[]{:S(2)}, u32[]{:S(2)}) collective-permute-start(f32[4,64,128]{2,1,0:T(8,128)S(1)} %get-tuple-element.38), channel_id=1, source_target_pairs={{0,2},{1,3},{2,0},{3,1},{4,6},{5,7},{6,4},{7,5},{8,10},{9,11},{10,... | collective-permute-start | bytes 393224 | tf_op jit(solution)/shard_map/ppermute | solution.py:347
  5.4 3.0 %shard_map.278 = (f32[12,64,128]{2,1,0:T(8,128)S(1)}, f32[12,64,128]{2,1,0:T(8,128)S(1)}, f32[12,64,128]{2,1,0:T(8,128)S(1)}, f32[12,64,128]{2,1,0:T(8,128)S(1)}) custom-call(s32[2]{0:T(128)S(1)} %pad_add_fusion.place_ref, f32[32,64,256]{2,1,0:T(8,128)} %rho_ref.3, bf16[4,64,256]{2,1,0:T(8,128)(2,1)} %constant.90.high_ref.sine_high_ref, ...), custom_call_target="tpu_custom_call" | custom-call | flops 1000000000 | bytes 4194304 | tf_op jit(solution)/shard_map/pallas_call | solution.py:241
  8.7 2.0 %collective-permute-start.4 = (f32[12,64,128]{2,1,0:T(8,128)S(1)}, f32[12,64,128]{2,1,0:T(8,128)S(1)}, u32[]{:S(2)}, u32[]{:S(2)}) collective-permute-start(f32[12,64,128]{2,1,0:T(8,128)S(1)} %get-tuple-element.43), channel_id=1, source_target_pairs={{0,2},{1,3},{2,0},{3,1},{4,6},{5,7},{6,4},{7,5},{8,10},{9,11},{10,... | collective-permute-start | bytes 1179656 | tf_op jit(solution)/shard_map/ppermute | solution.py:347
  10.6 14.2 %shard_map.276 = (f32[32,64,256]{2,1,0:T(8,128)S(1)}, f32[32,64,256]{2,1,0:T(8,128)S(1)}, f32[2,3072,128]{2,1,0:T(8,128)S(1)}, f32[8,256,256]{2,1,0:T(8,128)S(1)...) custom-call(s32[2]{0:T(128)S(1)} %pad_add_fusion.place_ref, ...), custom_call_target="tpu_custom_call" | custom-call | flops 10000000000 | bytes 4194304 | tf_op jit(solution)/shard_map/pallas_call | solution.py:241
  24.8 0.6 shard_map.277.refs_0_
  25.4 3.4 %collective-permute-done.5.refs_3_ = f32[12,64,128]{2,1,0:T(8,128)S(1)} collective-permute-done((f32[12,64,128]{2,1,0:T(8,128)S(1)}, f32[12,64,128]{2,1,0:T(8,128)S(1)}, u32[]{:S(2)}, u32[]{:S(2)}) %collective-permute-start.5) | collective-permute-done | bytes 393248 | tf_op jit(solution)/shard_map/ppermute | solution.py:347
  28.9 1.4 %shard_map.279.refs_1_ = f32[24,64,256]{2,1,0:T(8,128)S(1)} custom-call(f32[12,64,128]{2,1,0:T(8,128)S(1)} %get-tuple-element.41.refs_0_, f32[12,64,128]{2,1,0:T(8,128)S(1)} %collective-permute-done.3.refs_1_, f32[12,64,128]{2,1,0:T(8,128)S(1)} %collective-permute-done.4.refs_2_, f32[12,64,128]{2,1,0:T(8,128)S(1)} %collective-permute-done.5.refs_3_, ...), custom_call_target="tpu_custom_call" | custom-call | flops 1000000000 | bytes 4194304 | tf_op jit(solution)/shard_map/pallas_call | solution.py:241
  30.5 6.3 %shard_map.280 = (f32[32,64,256]{2,1,0:T(8,128)S(1)}, f32[32,1,384]{2,1,0:T(1,128)S(1)}, f32[8,128]{1,0:T(8,128)S(1)}) custom-call(s32[2]{0:T(128)S(1)} %pad_add_fusion.place_ref, f32[17,256]{1,0:T(8,128)S(1)} %copy-done.14, f32[8,64,256]{2,1,0:T(8,128)S(1)} %shard_map.277.refs_0_, f32[24,64,256]{2,1,0:T(8,128)S(1)} %shard_map.279.refs_1_, ...), custom_call_target="tpu_custom_call" | custom-call | flops 1000000000 | bytes 4194304 | tf_op jit(solution)/shard_map/pallas_call | solution.py:241
  36.8 13.0 %all_to_all.15.share_ref = f32[32,1,384]{2,1,0:T(1,128)S(1)} all-to-all(f32[32,1,384]{2,1,0:T(1,128)S(1)} %get-tuple-element.47), channel_id=1, replica_groups=mesh['gx'=8,'gy'=4] {'gx','gy'}, dimensions={0} | all-to-all | bytes 98304 | tf_op jit(solution)/shard_map/all_to_all | solution.py:733
  49.8 6.6 %shard_map.281 = (f32[32,64,256]{2,1,0:T(8,128)S(1)}, f32[8,4,8,256]{3,2,1,0:T(8,128)S(1)}, f32[8,128]{1,0:T(8,128)S(1)}) custom-call(s32[2]{0:T(128)S(1)} %pad_add_fusion.place_ref, f32[32,1,384]{2,1,0:T(1,128)S(1)} %all_to_all.15.share_ref, f32[8,384]{1,0:T(8,128)S(1)} %copy-done.15, f32[3,192,128]{2,1,0:T(8,128)S(1)} %get-tuple-element.48.unit_ref, ...), custom_call_target="tpu_custom_call" | custom-call | flops 1000000000 | bytes 4194304 | tf_op jit(solution)/shard_map/pallas_call | solution.py:241
  56.4 11.9 %all_to_all.16.near_ref = f32[8,4,8,256]{3,2,1,0:T(8,128)S(1)} all-to-all(f32[8,4,8,256]{3,2,1,0:T(8,128)S(1)} %get-tuple-element.52), channel_id=1, replica_groups=mesh['gx'=8,'gy'=4] {'gx'}, dimensions={0} | all-to-all | bytes 524288 | tf_op jit(solution)/shard_map/all_to_all | solution.py:904
  68.3 1.0 shard_map.282
  69.3 11.4 %all_to_all.17.ghost_ref = f32[8,24,256]{2,1,0:T(8,128)S(1)} all-to-all(f32[8,24,256]{2,1,0:T(8,128)S(1)} %shard_map.282), channel_id=1, replica_groups=mesh['gx'=8,'gy'=4] {'gx'}, dimensions={0} | all-to-all | bytes 393216 | tf_op jit(solution)/shard_map/all_to_all | solution.py:943
  80.8 0.7 shard_map.285
  81.5 1.6 %shard_map.284 = (f32[8,64,128]{2,1,0:T(8,128)S(1)}, f32[8,64,128]{2,1,0:T(8,128)S(1)}, f32[8,64,128]{2,1,0:T(8,128)S(1)}, f32[8,64,128]{2,1,0:T(8,128)S(1)}, f32[8,256]{1,0:T(8,128)}) custom-call(f32[32,64,256]{2,1,0:T(8,128)S(1)} %get-tuple-element.50.total_ref, f32[32,64,256]{2,1,0:T(8,128)S(1)} %get-tuple-element.51.profile_ref, ...), custom_call_target="tpu_custom_call" | custom-call | flops 1000000000 | bytes 4194304 | tf_op jit(solution)/shard_map/pallas_call | solution.py:241
  83.1 0.5 collective-permute-start.9
  84.0 0.9 collective-permute-start.11
  84.9 0.8 collective-permute-start.17
  85.8 10.9 %collective-permute-done.17.refs_9_ = f32[8,256]{1,0:T(8,128)S(1)} collective-permute-done((f32[8,256]{1,0:T(8,128)S(1)}, f32[8,256]{1,0:T(8,128)S(1)}, u32[]{:S(2)}, u32[]{:S(2)}) %collective-permute-start.17) | collective-permute-done | bytes 8224 | tf_op jit(solution)/shard_map/ppermute | solution.py:347
  96.6 0.5 collective-permute-start.13
  97.1 1.6 %collective-permute-start.14 = (f32[4,64,128]{2,1,0:T(8,128)S(1)}, f32[4,64,128]{2,1,0:T(8,128)S(1)}, u32[]{:S(2)}, u32[]{:S(2)}) collective-permute-start(f32[4,64,128]{2,1,0:T(8,128)S(1)} %get-tuple-element.68), channel_id=1, source_target_pairs={{0,3},{1,2},{2,1},{3,0},{4,7},{5,6},{6,5},{7,4},{8,11},{9,10},{10,... | collective-permute-start | bytes 393224 | tf_op jit(solution)/shard_map/ppermute | solution.py:347
  98.8 1.1 shard_map.283
  99.9 3.1 %collective-permute-done.13.refs_2_ = f32[4,64,128]{2,1,0:T(8,128)S(1)} collective-permute-done((f32[4,64,128]{2,1,0:T(8,128)S(1)}, f32[4,64,128]{2,1,0:T(8,128)S(1)}, u32[]{:S(2)}, u32[]{:S(2)}) %collective-permute-start.13) | collective-permute-done | bytes 131104 | tf_op jit(solution)/shard_map/ppermute | solution.py:347
  103.0 2.4 %collective-permute-done.14.refs_3_ = f32[4,64,128]{2,1,0:T(8,128)S(1)} collective-permute-done((f32[4,64,128]{2,1,0:T(8,128)S(1)}, f32[4,64,128]{2,1,0:T(8,128)S(1)}, u32[]{:S(2)}, u32[]{:S(2)}) %collective-permute-start.14) | collective-permute-done | bytes 131104 | tf_op jit(solution)/shard_map/ppermute | solution.py:347
  105.9 1.0 collective-permute-start.8
  106.9 1.2 %shard_map.286.refs_5_ = f32[32,64,256]{2,1,0:T(8,128)} custom-call(f32[4,64,128]{2,1,0:T(8,128)S(1)} %get-tuple-element.65.refs_0_, f32[4,64,128]{2,1,0:T(8,128)S(1)} %collective-permute-done.12.refs_1_, f32[4,64,128]{2,1,0:T(8,128)S(1)} %collective-permute-done.13.refs_2_, f32[4,64,128]{2,1,0:T(8,128)S(1)} %collective-permute-done.14.refs_3_, ...), custom_call_target="tpu_custom_call" | custom-call | flops 1000000000 | bytes 4194304 | tf_op jit(solution)/shard_map/pallas_call | solution.py:241
  108.1 0.6 collective-permute-start.16
  109.0 1.6 %shard_map.287.refs_5_ = f32[32,64,256]{2,1,0:T(8,128)} custom-call(f32[8,64,128]{2,1,0:T(8,128)S(1)} %get-tuple-element.61.refs_0_, f32[8,64,128]{2,1,0:T(8,128)S(1)} %collective-permute-done.9.refs_1_, f32[8,64,128]{2,1,0:T(8,128)S(1)} %collective-permute-done.10.refs_2_, ...), custom_call_target="tpu_custom_call", output_to_operand_aliasing={{}: (5, {})} | custom-call | flops 1000000000 | bytes 4194304 | tf_op jit(solution)/shard_map/pallas_call | solution.py:241
  110.6 3.3 %collective-permute-done.16.refs_8_ = f32[8,256]{1,0:T(8,128)S(1)} collective-permute-done((f32[8,256]{1,0:T(8,128)S(1)}, f32[8,256]{1,0:T(8,128)S(1)}, u32[]{:S(2)}, u32[]{:S(2)}) %collective-permute-start.16) | collective-permute-done | bytes 8224 | tf_op jit(solution)/shard_map/ppermute | solution.py:347
  114.0 1.2 %shard_map.288 = (f32[32,64,256]{2,1,0:T(8,128)}, f32[2]{0:T(128)}) custom-call(f32[4,64,128]{2,1,0:T(8,128)S(1)} %get-tuple-element.56.refs_0_, f32[4,64,128]{2,1,0:T(8,128)S(1)} %collective-permute-done.6.refs_1_, f32[4,64,128]{2,1,0:T(8,128)S(1)} %collective-permute-done.7.refs_2_, ...), custom_call_target="tpu_custom_call", output_to_operand_aliasing={{0}: (5, {})} | custom-call | flops 1000000000 | bytes 4194304 | tf_op jit(solution)/shard_map/pallas_call | solution.py:241
  (56 shorter events, 1.7 us)
Async XLA Ops:
  2.2 8.4 %collective-permute-start = (f32[4,64,128]{2,1,0:T(8,128)S(1)}, f32[4,64,128]{2,1,0:T(8,128)S(1)}, u32[]{:S(2)}, u32[]{:S(2)}) collective-permute-start(f32[4,64,128]{2,1,0:T(8,128)S(1)} %get-tuple-element.37), channel_id=1, source_target_pairs={{0,1},{1,0},{2,3},{3,2},{4,5},{5,4},{6,7},{7,6},{8,9},{9,8},{10,11... | collective-permute-start | bytes 393224 | tf_op jit(solution)/shard_map/ppermute | solution.py:347
  2.8 22.0 %collective-permute-start.1 = (f32[4,64,128]{2,1,0:T(8,128)S(1)}, f32[4,64,128]{2,1,0:T(8,128)S(1)}, u32[]{:S(2)}, u32[]{:S(2)}) collective-permute-start(f32[4,64,128]{2,1,0:T(8,128)S(1)} %get-tuple-element.38), channel_id=1, source_target_pairs={{0,2},{1,3},{2,0},{3,1},{4,6},{5,7},{6,4},{7,5},{8,10},{9,11},{10,... | collective-permute-start | bytes 393224 | tf_op jit(solution)/shard_map/ppermute | solution.py:347
  5.4 19.5 %collective-permute-start.2 = (f32[4,64,128]{2,1,0:T(8,128)S(1)}, f32[4,64,128]{2,1,0:T(8,128)S(1)}, u32[]{:S(2)}, u32[]{:S(2)}) collective-permute-start(f32[4,64,128]{2,1,0:T(8,128)S(1)} %get-tuple-element.39), channel_id=1, source_target_pairs={{0,3},{1,2},{2,1},{3,0},{4,7},{5,6},{6,5},{7,4},{8,11},{9,10},{10,... | collective-permute-start | bytes 393224 | tf_op jit(solution)/shard_map/ppermute | solution.py:347
  8.4 17.0 %collective-permute-start.3 = (f32[12,64,128]{2,1,0:T(8,128)S(1)}, f32[12,64,128]{2,1,0:T(8,128)S(1)}, u32[]{:S(2)}, u32[]{:S(2)}) collective-permute-start(f32[12,64,128]{2,1,0:T(8,128)S(1)} %get-tuple-element.42), channel_id=1, source_target_pairs={{0,1},{1,0},{2,3},{3,2},{4,5},{5,4},{6,7},{7,6},{8,9},{9,8},{10,11... | collective-permute-start | bytes 1179656 | tf_op jit(solution)/shard_map/ppermute | solution.py:347
  8.7 16.8 %collective-permute-start.4 = (f32[12,64,128]{2,1,0:T(8,128)S(1)}, f32[12,64,128]{2,1,0:T(8,128)S(1)}, u32[]{:S(2)}, u32[]{:S(2)}) collective-permute-start(f32[12,64,128]{2,1,0:T(8,128)S(1)} %get-tuple-element.43), channel_id=1, source_target_pairs={{0,2},{1,3},{2,0},{3,1},{4,6},{5,7},{6,4},{7,5},{8,10},{9,11},{10,... | collective-permute-start | bytes 1179656 | tf_op jit(solution)/shard_map/ppermute | solution.py:347
  10.6 18.2 %collective-permute-start.5 = (f32[12,64,128]{2,1,0:T(8,128)S(1)}, f32[12,64,128]{2,1,0:T(8,128)S(1)}, u32[]{:S(2)}, u32[]{:S(2)}) collective-permute-start(f32[12,64,128]{2,1,0:T(8,128)S(1)} %get-tuple-element.44), channel_id=1, source_target_pairs={{0,3},{1,2},{2,1},{3,0},{4,7},{5,6},{6,5},{7,4},{8,11},{9,10},{10,... | collective-permute-start | bytes 1179656 | tf_op jit(solution)/shard_map/ppermute | solution.py:347
  28.9 1.5 %copy-start.3 = (bf16[2,128,256]{2,1,0:T(8,128)(2,1)S(1)}, bf16[2,128,256]{2,1,0:T(8,128)(2,1)}, u32[]{:S(2)}) copy-start(bf16[2,128,256]{2,1,0:T(8,128)(2,1)} %constant.92.refs_8_) | copy-start | bytes 393220
  28.9 1.5 %copy-start.8 = (bf16[256,128]{1,0:T(8,128)(2,1)S(1)}, bf16[256,128]{1,0:T(8,128)(2,1)}, u32[]{:S(2)}) copy-start(bf16[256,128]{1,0:T(8,128)(2,1)} %constant.77.clone.refs_5_) | copy-start | bytes 196612
  28.9 1.5 %copy-start.9 = (bf16[256,128]{1,0:T(8,128)(2,1)S(1)}, bf16[256,128]{1,0:T(8,128)(2,1)}, u32[]{:S(2)}) copy-start(bf16[256,128]{1,0:T(8,128)(2,1)} %constant.76.clone.refs_4_) | copy-start | bytes 196612
  28.9 1.5 %copy-start.10 = (f32[2,24,256]{2,1,0:T(8,128)S(1)}, f32[2,24,256]{2,1,0:T(8,128)}, u32[]{:S(2)}) copy-start(f32[2,24,256]{2,1,0:T(8,128)} %constant.83.clone.refs_9_) | copy-start | bytes 147460
  28.9 1.5 %copy-start.11 = (f32[3,8,384]{2,1,0:T(8,128)S(1)}, f32[3,8,384]{2,1,0:T(8,128)}, u32[]{:S(2)}) copy-start(f32[3,8,384]{2,1,0:T(8,128)} %constant.84.clone.refs_12_) | copy-start | bytes 110596
  28.9 1.5 %copy-start.12 = (bf16[4,1,24,64]{3,2,1,0:T(8,128)(2,1)S(1)}, bf16[4,1,24,64]{3,2,1,0:T(8,128)(2,1)}, u32[]{:S(2)}) copy-start(bf16[4,1,24,64]{3,2,1,0:T(8,128)(2,1)} %constant.79.clone.refs_7_) | copy-start | bytes 36868
  28.9 1.5 %copy-start.13 = (bf16[4,1,24,64]{3,2,1,0:T(8,128)(2,1)S(1)}, bf16[4,1,24,64]{3,2,1,0:T(8,128)(2,1)}, u32[]{:S(2)}) copy-start(bf16[4,1,24,64]{3,2,1,0:T(8,128)(2,1)} %constant.78.clone.refs_6_) | copy-start | bytes 36868
  30.4 19.3 %copy-start.2 = (f32[2,256,128]{2,1,0:T(8,128)S(1)}, f32[2,256,128]{2,1,0:T(8,128)}, u32[]{:S(2)}) copy-start(f32[2,256,128]{2,1,0:T(8,128)} %constant.75.clone.column_ref) | copy-start | bytes 786436
  30.4 19.3 %copy-start.4 = (bf16[4,64,256]{2,1,0:T(8,128)(2,1)S(1)}, bf16[4,64,256]{2,1,0:T(8,128)(2,1)}, u32[]{:S(2)}) copy-start(bf16[4,64,256]{2,1,0:T(8,128)(2,1)} %constant.89.clone.local_low_ref) | copy-start | bytes 393220
  30.5 19.3 %copy-start.5 = (bf16[4,64,256]{2,1,0:T(8,128)(2,1)S(1)}, bf16[4,64,256]{2,1,0:T(8,128)(2,1)}, u32[]{:S(2)}) copy-start(bf16[4,64,256]{2,1,0:T(8,128)(2,1)} %constant.88.clone.local_high_ref) | copy-start | bytes 393220
  30.5 19.3 %copy-start.6 = (bf16[256,256]{1,0:T(8,128)(2,1)S(1)}, bf16[256,256]{1,0:T(8,128)(2,1)}, u32[]{:S(2)}) copy-start(bf16[256,256]{1,0:T(8,128)(2,1)} %constant.87.clone.folded_low_ref) | copy-start | bytes 393220
  30.5 19.3 %copy-start.7 = (bf16[256,256]{1,0:T(8,128)(2,1)S(1)}, bf16[256,256]{1,0:T(8,128)(2,1)}, u32[]{:S(2)}) copy-start(bf16[256,256]{1,0:T(8,128)(2,1)} %constant.86.clone.folded_high_ref) | copy-start | bytes 393220
  30.5 19.3 %copy-start.15 = (f32[8,384]{1,0:T(8,128)S(1)}, f32[8,384]{1,0:T(8,128)}, u32[]{:S(2)}) copy-start(f32[8,384]{1,0:T(8,128)} %constant.85.clone.scale_ref) | copy-start | bytes 36868
  30.5 19.3 %copy-start.16 = (f32[8,256]{1,0:T(8,128)S(1)}, f32[8,256]{1,0:T(8,128)}, u32[]{:S(2)}) copy-start(f32[8,256]{1,0:T(8,128)} %constant.74.clone.row_ref) | copy-start | bytes 24580
  81.4 15.7 %collective-permute-start.12 = (f32[4,64,128]{2,1,0:T(8,128)S(1)}, f32[4,64,128]{2,1,0:T(8,128)S(1)}, u32[]{:S(2)}, u32[]{:S(2)}) collective-permute-start(f32[4,64,128]{2,1,0:T(8,128)S(1)} %get-tuple-element.66), channel_id=1, source_target_pairs={{0,1},{1,0},{2,3},{3,2},{4,5},{5,4},{6,7},{7,6},{8,9},{9,8},{10,11... | collective-permute-start | bytes 393224 | tf_op jit(solution)/shard_map/ppermute | solution.py:347
  83.1 22.8 %collective-permute-start.9 = (f32[8,64,128]{2,1,0:T(8,128)S(1)}, f32[8,64,128]{2,1,0:T(8,128)S(1)}, u32[]{:S(2)}, u32[]{:S(2)}) collective-permute-start(f32[8,64,128]{2,1,0:T(8,128)S(1)} %get-tuple-element.62), channel_id=1, source_target_pairs={{0,1},{1,0},{2,3},{3,2},{4,5},{5,4},{6,7},{7,6},{8,9},{9,8},{10,11... | collective-permute-start | bytes 786440 | tf_op jit(solution)/shard_map/ppermute | solution.py:347
  83.6 24.5 %collective-permute-start.10 = (f32[8,64,128]{2,1,0:T(8,128)S(1)}, f32[8,64,128]{2,1,0:T(8,128)S(1)}, u32[]{:S(2)}, u32[]{:S(2)}) collective-permute-start(f32[8,64,128]{2,1,0:T(8,128)S(1)} %get-tuple-element.63), channel_id=1, source_target_pairs={{0,2},{1,3},{2,0},{3,1},{4,6},{5,7},{6,4},{7,5},{8,10},{9,11},{10,... | collective-permute-start | bytes 786440 | tf_op jit(solution)/shard_map/ppermute | solution.py:347
  84.0 24.6 %collective-permute-start.11 = (f32[8,64,128]{2,1,0:T(8,128)S(1)}, f32[8,64,128]{2,1,0:T(8,128)S(1)}, u32[]{:S(2)}, u32[]{:S(2)}) collective-permute-start(f32[8,64,128]{2,1,0:T(8,128)S(1)} %get-tuple-element.64), channel_id=1, source_target_pairs={{0,3},{1,2},{2,1},{3,0},{4,7},{5,6},{6,5},{7,4},{8,11},{9,10},{10,... | collective-permute-start | bytes 786440 | tf_op jit(solution)/shard_map/ppermute | solution.py:347
  84.9 11.7 %collective-permute-start.17 = (f32[8,256]{1,0:T(8,128)S(1)}, f32[8,256]{1,0:T(8,128)S(1)}, u32[]{:S(2)}, u32[]{:S(2)}) collective-permute-start(f32[8,256]{1,0:T(8,128)S(1)} %get-tuple-element.69.refs_6_), channel_id=1, source_target_pairs={{0,3},{1,2},{2,1},{3,0},{4,7},{5,6},{6,5},{7,4},{8,11},{9,10},{10,... | collective-permute-start | bytes 24584 | tf_op jit(solution)/shard_map/ppermute | solution.py:347
  96.6 6.4 %collective-permute-start.13 = (f32[4,64,128]{2,1,0:T(8,128)S(1)}, f32[4,64,128]{2,1,0:T(8,128)S(1)}, u32[]{:S(2)}, u32[]{:S(2)}) collective-permute-start(f32[4,64,128]{2,1,0:T(8,128)S(1)} %get-tuple-element.67), channel_id=1, source_target_pairs={{0,2},{1,3},{2,0},{3,1},{4,6},{5,7},{6,4},{7,5},{8,10},{9,11},{10,... | collective-permute-start | bytes 393224 | tf_op jit(solution)/shard_map/ppermute | solution.py:347
  97.1 8.3 %collective-permute-start.14 = (f32[4,64,128]{2,1,0:T(8,128)S(1)}, f32[4,64,128]{2,1,0:T(8,128)S(1)}, u32[]{:S(2)}, u32[]{:S(2)}) collective-permute-start(f32[4,64,128]{2,1,0:T(8,128)S(1)} %get-tuple-element.68), channel_id=1, source_target_pairs={{0,3},{1,2},{2,1},{3,0},{4,7},{5,6},{6,5},{7,4},{8,11},{9,10},{10,... | collective-permute-start | bytes 393224 | tf_op jit(solution)/shard_map/ppermute | solution.py:347
  103.0 10.9 %collective-permute-start.6 = (f32[4,64,128]{2,1,0:T(8,128)S(1)}, f32[4,64,128]{2,1,0:T(8,128)S(1)}, u32[]{:S(2)}, u32[]{:S(2)}) collective-permute-start(f32[4,64,128]{2,1,0:T(8,128)S(1)} %get-tuple-element.57), channel_id=1, source_target_pairs={{0,1},{1,0},{2,3},{3,2},{4,5},{5,4},{6,7},{7,6},{8,9},{9,8},{10,11... | collective-permute-start | bytes 393224 | tf_op jit(solution)/shard_map/ppermute | solution.py:347
  105.4 8.5 %collective-permute-start.7 = (f32[4,64,128]{2,1,0:T(8,128)S(1)}, f32[4,64,128]{2,1,0:T(8,128)S(1)}, u32[]{:S(2)}, u32[]{:S(2)}) collective-permute-start(f32[4,64,128]{2,1,0:T(8,128)S(1)} %get-tuple-element.58), channel_id=1, source_target_pairs={{0,2},{1,3},{2,0},{3,1},{4,6},{5,7},{6,4},{7,5},{8,10},{9,11},{10,... | collective-permute-start | bytes 393224 | tf_op jit(solution)/shard_map/ppermute | solution.py:347
  105.9 8.1 %collective-permute-start.8 = (f32[4,64,128]{2,1,0:T(8,128)S(1)}, f32[4,64,128]{2,1,0:T(8,128)S(1)}, u32[]{:S(2)}, u32[]{:S(2)}) collective-permute-start(f32[4,64,128]{2,1,0:T(8,128)S(1)} %get-tuple-element.59), channel_id=1, source_target_pairs={{0,3},{1,2},{2,1},{3,0},{4,7},{5,6},{6,5},{7,4},{8,11},{9,10},{10,... | collective-permute-start | bytes 393224 | tf_op jit(solution)/shard_map/ppermute | solution.py:347
  108.1 5.8 %collective-permute-start.16 = (f32[8,256]{1,0:T(8,128)S(1)}, f32[8,256]{1,0:T(8,128)S(1)}, u32[]{:S(2)}, u32[]{:S(2)}) collective-permute-start(f32[8,256]{1,0:T(8,128)S(1)} %get-tuple-element.69.refs_6_), channel_id=1, source_target_pairs={{0,2},{1,3},{2,0},{3,1},{4,6},{5,7},{6,4},{7,5},{8,10},{9,11},{10,... | collective-permute-start | bytes 24584 | tf_op jit(solution)/shard_map/ppermute | solution.py:347
  108.7 5.3 %collective-permute-start.15 = (f32[8,256]{1,0:T(8,128)S(1)}, f32[8,256]{1,0:T(8,128)S(1)}, u32[]{:S(2)}, u32[]{:S(2)}) collective-permute-start(f32[8,256]{1,0:T(8,128)S(1)} %get-tuple-element.69.refs_6_), channel_id=1, source_target_pairs={{0,1},{1,0},{2,3},{3,2},{4,5},{5,4},{6,7},{7,6},{8,9},{9,8},{10,11... | collective-permute-start | bytes 24584 | tf_op jit(solution)/shard_map/ppermute | solution.py:347
  (3 other events, 4.5 us)
where the time goes:
time: 116 us; the launch traced here: 115 us
  Pallas kernels  42 us (36%)
  blocking collectives  36.3 us (31%)
  waiting for transfers between devices  23.2 us (20%)
  starting transfers between devices  12.5 us (11%)
    pallas_call x14, Pallas kernels, run(): return kernel(*placed)  42 us
    ppermute x18, waiting for transfers between devices, exchange(): received.append(lax.ppermute(parts[shift], 'gy', ring))  23.2 us
    all_to_all x1, blocking collectives, shards(): shared = lax.all_to_all(moments, ('gx', 'gy'), 0, 0, tiled=True)  13 us
    ppermute x18, starting transfers between devices, exchange(): received.append(lax.ppermute(parts[shift], 'gy', ring))  12.5 us
    all_to_all x1, blocking collectives, shards(): gathered = lax.all_to_all(nears, 'gx', 0, 0, tiled=True)  11.9 us
    all_to_all x1, blocking collectives, shards(): returned = lax.all_to_all(answers, 'gx', 0, 0, tiled=True)  11.4 us
  transfers between devices with their start and end apart: 18, of which 5 were waited for; matrix products, arithmetic and copies ran while one was open for 0% of the time, Pallas kernels for 20%

commit v1 on v0

--- a/solution.py
+++ b/solution.py
@@ -12,6 +12,7 @@
 ORDER = 16
 COUNT = ORDER + 1
 PAIRS = 256
+NEWTON = 1
 FACE_ROWS = 16
 TERMS = 384
 outer_ratio = 1.1
@@ -60,8 +61,9 @@
 
 def inverted(value):
     guess = pl.reciprocal(value, approx=True)
-    guess = guess * (2.0 - value * guess)
-    return guess * (2.0 - value * guess)
+    for _ in range(NEWTON):
+        guess = guess * (2.0 - value * guess)
+    return guess
 
 
 def exact(left, right, dims):
@@ -124,10 +126,12 @@
             for spot, pair in enumerate(pair_list()):
                 maps[face, spot, column] = scale * expansion[pair] / radius_scale**degree
     masks = np.zeros((3, 8, TERMS))
-    for column, (kind, l, m) in enumerate(terms):
+    for column, (kind, m, odd, _) in enumerate(power_list()):
         masks[0, (m + kind) % 2, column] = 1.0
         masks[1, kind, column] = 1.0
-        masks[2, (l - m) % 2, column] = 1.0
+        masks[2, odd, column] = 1.0
+    used = len(terms)
+    maps[:, :, :used] = maps[:, :, :used] @ power_weights()
     folded = np.zeros((2, length // 2, length))
     parity = np.arange(length) % 2
     upper = 2.0 * sine[length // 2 :]
@@ -148,36 +152,53 @@
     )
 
 
-def evaluation_scales():
-    sector, running = [1.0], 1.0
-    for l in range(1, COUNT):
-        running *= math.sqrt((2 * l - 1) / (2.0 * l)) if l > 1 else 1.0
-        sector.append(running)
-    kappa, beta = {}, {}
+def power_list():
+    return [
+        (kind, m, odd, power)
+        for kind in range(2)
+        for m in range(kind, COUNT)
+        for odd in range(2)
+        for power in range((ORDER - m - odd) // 2 + 1)
+        if m + odd <= ORDER
+    ]
+
+
+def power_weights():
+    poly = np.polynomial.polynomial
+    columns = {term: spot for spot, term in enumerate(power_list())}
+    harmonics, sector = {}, 1.0
     for m in range(COUNT):
-        kappa[m, m] = sector[m]
-        previous = 1.0
+        if m > 1:
+            sector *= math.sqrt((2 * m - 1) / (2.0 * m))
+        harmonics[m, m] = np.array([sector])
         for l in range(m + 1, COUNT):
-            near = (2 * l - 1) / math.sqrt(l * l - m * m)
-            far = math.sqrt((l - 1) ** 2 - m * m) / math.sqrt(l * l - m * m)
-            kappa[l, m] = kappa[l - 1, m] * near
-            beta[l, m] = far / (near * previous) if l >= m + 2 else 0.0
-            previous = near
-    scales = np.zeros((8, TERMS))
-    for row, (_, l, m) in enumerate(term_list()):
-        factor = 1.0 if m == 0 else 2.0
-        weight = factor / (4.0 * math.pi * radius_scale * outer_ratio ** (l + 1))
-        scales[:, row] = weight * kappa[l, m]
-    return scales, beta
+            value = (2 * l - 1) * poly.polymul([0.0, 1.0], harmonics[l - 1, m])
+            if l >= m + 2:
+                value = poly.polysub(value, math.sqrt((l - 1) ** 2 - m * m) * harmonics[l - 2, m])
+            harmonics[l, m] = value / math.sqrt(l * l - m * m)
+    table = np.zeros((len(term_list()), len(columns)))
+    for row, (kind, l, m) in enumerate(term_list()):
+        odd = (l - m) % 2
+        inner = harmonics[l, m][odd::2]
+        shifted = np.zeros(1)
+        for value in inner[::-1]:
+            shifted = poly.polyadd(poly.polymul(shifted, [0.5, 0.5]), [value])
+        factor = (1.0 if m == 0 else 2.0) / (4.0 * math.pi * radius_scale)
+        for power in range(len(inner)):
+            table[row, columns[kind, m, odd, power]] = (
+                factor * shifted[power] / outer_ratio ** (l + 1)
+            )
+    return table
 
 
 def evaluate(coef, unit_x, unit_y, unit_z):
-    beta = evaluation_scales()[1]
-    rows = {term: row for row, term in enumerate(term_list())}
+    rows = {term: row for row, term in enumerate(power_list())}
+    shifted = 2.0 * unit_z * unit_z - 1.0
     total = {}
 
-    def add(key, value):
-        total[key] = value if key not in total else total[key] + value
+    def weight(*term):
+        row = rows[term]
+        return jnp.broadcast_to(coef[row : row + 1, :], unit_z.shape)
 
     cosine, sine = None, None
     for m in range(COUNT):
@@ -185,30 +206,19 @@
             cosine, sine = unit_x, unit_y
         elif m > 1:
             cosine, sine = unit_x * cosine - unit_y * sine, unit_x * sine + unit_y * cosine
-        sums = {}
-        older, newer = None, None
-        for l in range(m, COUNT):
-            if l == m:
-                now = None
-            elif l == m + 1:
-                now = unit_z
-            elif l == m + 2:
-                now = unit_z * newer - beta[l, m]
-            else:
-                now = unit_z * newer - beta[l, m] * older
-            for kind in range(1 if m == 0 else 2):
-                row = rows[kind, l, m]
-                weight = coef[row : row + 1, :]
-                weight = jnp.broadcast_to(weight, unit_z.shape)
-                term = weight if now is None else weight * now
-                key = (kind, (l - m) % 2)
-                sums[key] = term if key not in sums else sums[key] + term
-            older, newer = newer, now
-        for (kind, odd), value in sums.items():
-            if m > 0:
-                value = value * (cosine, sine)[kind]
-            add((m % 2, kind, odd), value)
-    return total
+        for kind in range(1 if m == 0 else 2):
+            for odd in range(2):
+                if m + odd > ORDER:
+                    continue
+                top = (ORDER - m - odd) // 2
+                value = weight(kind, m, odd, top)
+                for power in range(top - 1, -1, -1):
+                    value = value * shifted + weight(kind, m, odd, power)
+                if m > 0:
+                    value = value * (cosine, sine)[kind]
+                key = (m % 2, kind, odd)
+                total[key] = total[key] + value if key in total else value
+    return {key: value * unit_z if key[2] else value for key, value in total.items()}
 
 
 RESIDENT = pl.BlockSpec(memory_space=pltpu.VMEM)
@@ -274,7 +284,7 @@
     sine_low = sine_low.reshape(groups_y, cells_b, length)
     parts_in = tiles // 4 if tiles % 4 == 0 else tiles
     uneven = parts_in < tiles
-    going = [parts_in, 3 * parts_in] if uneven else [tiles]
+    going = [parts_in, 2 * parts_in, parts_in] if uneven else [tiles]
     coming = [parts_in, 2 * parts_in, parts_in] if uneven else [tiles]
 
     def starts_of(portions):
@@ -364,7 +374,13 @@
     for slab in range(groups_x):
         spots += [slab * cells_a, (slab + 1) * cells_a + 1]
     green_lines = lines[spots]
-    green = (scale * green_lines[:, None, :] * green_lines[None, :, :]).reshape(-1, length)
+    chosen, green_row = [], {}
+    for low in range(1, ghosts - 1):
+        for high in range(low, ghosts - 1):
+            green_row[low, high] = green_row[high, low] = len(chosen)
+            chosen.append(scale * green_lines[low] * green_lines[high])
+    chosen += [np.zeros(length)] * (-len(chosen) % 16)
+    green = np.stack(chosen)
     eigen_column = np.broadcast_to(tabs["eigen"][:, None], (length, length))
     eigen_row = np.broadcast_to(tabs["eigen"][None, :], (8, length))
     cell_column = np.broadcast_to(tabs["cells"][:, None], (length, half))
@@ -493,7 +509,7 @@
             field,
             field,
             kept(length // 128, depth * 2 * hat_pad, 128),
-            kept(modes, ghosts * ghosts, length),
+            kept(modes, green.shape[0], length),
             kept(3, 2 * cells_a + half, half),
             pltpu.VMEM((2, groups_y * lanes, wide), BF16),
             pltpu.VMEM((2, length, length), BF16),
@@ -517,7 +533,6 @@
     lookup = lookup.reshape(groups_y, 24, blocks, block).transpose(0, 2, 1, 3)
     lookup_high, lookup_low = (jnp.asarray(t) for t in split_np(lookup))
     spread = jnp.asarray(tabs["spread"].astype(np.float32)).astype(BF16)
-    map_high, map_low = (jnp.asarray(t) for t in split_np(tabs["maps"]))
     factors, profile, probe_table, green_table, units, pairs, table = tables
 
     def second_body(*refs):
@@ -567,8 +582,7 @@
             lookup_low_ref,
             spread_ref,
             own_ref,
-            map_high_ref,
-            map_low_ref,
+            map_ref,
             mask_ref,
             field_ref,
             moment_ref,
@@ -698,16 +712,14 @@
                         answer = mul(high, spread_ref[1], NN) + mul(low, spread_ref[1], NN)
                         value = jnp.sum(answer * own_ref[0], axis=0, keepdims=True)
                     stack = jnp.where(rows == parity, value, stack)
-                moments = moments + triple(stack, map_high_ref[face], map_low_ref[face], NN) * (
-                    mask_ref[face]
-                )
+                moments = moments + exact(stack, map_ref[face], NN) * mask_ref[face]
             moments = jnp.sum(moments, axis=0, keepdims=True)
             moment_ref[...] = jnp.broadcast_to(moments[None], moment_ref.shape)
 
     solved, moments, energy_one = call(
         solve_body,
         (blocks,),
-        [SCALARS] * 2 + [RESIDENT] * (len(going) + 11),
+        [SCALARS] * 2 + [RESIDENT] * (len(going) + 10),
         [RESIDENT] * 3,
         [field, kept(devices, 1, TERMS), kept(8, 128)],
         [
@@ -726,13 +738,11 @@
         lookup_low,
         spread,
         const("own"),
-        map_high,
-        map_low,
+        const("maps"),
         const("masks"),
     )
     shared = lax.all_to_all(moments, ("gx", "gy"), 0, 0, tiled=True)
 
-    scales = jnp.asarray(evaluation_scales()[0].astype(np.float32))
     folded_high, folded_low = (jnp.asarray(t) for t in split_np(tabs["folded"]))
     local_high, local_low = (
         jnp.asarray(np.ascontiguousarray(t.T).reshape(groups_y, depth, length))
@@ -745,7 +755,6 @@
     def source_body(
         place_ref,
         share_ref,
-        scale_ref,
         unit_ref,
         folded_high_ref,
         folded_low_ref,
@@ -777,7 +786,7 @@
         @pl.when(step == 0)
         def _():
             ones = jnp.full((8, 128), 0.125, F32)
-            shares = jnp.sum(share_ref[...], axis=0) * scale_ref[...]
+            shares = jnp.broadcast_to(jnp.sum(share_ref[...], axis=0), (8, TERMS))
             coef[...] = exact(shares, ones, TN)
             energy_ref[...] = jnp.zeros_like(energy_ref)
 
@@ -872,7 +881,7 @@
     total, nears, energy_two = call(
         source_body,
         (blocks,),
-        [SCALARS] + [RESIDENT] * 11,
+        [SCALARS] + [RESIDENT] * 10,
         [RESIDENT] * 3,
         [field, kept(groups_x, 4, modes, length), kept(8, 128)],
         [
@@ -889,7 +898,6 @@
     )(
         place,
         shared,
-        scales,
         units,
         folded_high,
         folded_low,
@@ -918,11 +926,16 @@
                 if 0 <= neighbour < groups_x:
                     value = (first if side else last)[neighbour]
                     other = (other_first if side else other_last)[neighbour]
-                    base = (2 * slab + side) * ghosts
                     for s in range(groups_x):
-                        near, far = green_ref[:, base + 2 * s, :], green_ref[:, base + 2 * s + 1, :]
-                        value = value + near * first[s] + far * last[s]
-                        other = other + near * other_first[s] + far * other_last[s]
+                        for end, one, two in (
+                            (0, first, other_first),
+                            (1, last, other_last),
+                        ):
+                            row = green_row.get((2 * slab + side, 2 * s + end))
+                            if row is not None:
+                                green = green_ref[:, row, :]
+                                value = value + green * one[s]
+                                other = other + green * two[s]
                 energy_one = energy_one + value * (last if side else first)[slab]
                 energy_two = energy_two + value * (other_last if side else other_first)[slab]
                 out_ref[slab, side * modes : (side + 1) * modes, :] = value + other

time: 116 us -> 116 us (level)
  starting transfers between devices: 12.5 us -> 16.9 us
  Pallas kernels: 42 us -> 39.5 us
  waiting for transfers between devices: 23.2 us -> 21.5 us
    ppermute x18 -> x21, starting transfers between devices: 12.5 us -> 16.9 us  [exchange(): received.append(lax.ppermute(parts[shift], 'gy', ring))]
    pallas_call x14 -> x16, Pallas kernels: 42 us -> 39.5 us  [run(): return kernel(*placed)]
    ppermute x18 -> x21, waiting for transfers between devices: 23.2 us -> 21.5 us  [exchange(): received.append(lax.ppermute(parts[shift], 'gy', ring))]
  transfers between devices with their start and end apart: 18 -> 21, of which waited for: 5 -> 7; matrix products, arithmetic and copies ran while one was open for 0% -> 0% of each run, Pallas kernels for 20% -> 19%
where the time goes in v1:
time: 116 us
  Pallas kernels  39.5 us (34%)
  blocking collectives  36.8 us (32%)
  waiting for transfers between devices  21.5 us (19%)
  starting transfers between devices  16.9 us (15%)
  between operations  1.16 us (1%)
    pallas_call x16, Pallas kernels, run(): return kernel(*placed)  39.5 us
    ppermute x21, waiting for transfers between devices, exchange(): received.append(lax.ppermute(parts[shift], 'gy', ring))  21.5 us
    ppermute x21, starting transfers between devices, exchange(): received.append(lax.ppermute(parts[shift], 'gy', ring))  16.9 us
    all_to_all x1, blocking collectives, shards(): shared = lax.all_to_all(moments, ('gx', 'gy'), 0, 0, tiled=True)  13.3 us
    all_to_all x1, blocking collectives, shards(): gathered = lax.all_to_all(nears, 'gx', 0, 0, tiled=True)  12.1 us
    all_to_all x1, blocking collectives, shards(): returned = lax.all_to_all(answers, 'gx', 0, 0, tiled=True)  11.4 us
  transfers between devices with their start and end apart: 21, of which 7 were waited for; matrix products, arithmetic and copies ran while one was open for 0% of the time, Pallas kernels for 19%

profile of v1, /device:TPU:0, one launch (start us, length us, event | category | flops | bytes accessed | tf_op | source)
XLA Modules:
  0.0 116.1 jit_solution(7407700039342519181)
XLA Ops:
  0.7 1.5 %shard_map.257 = (f32[4,64,128]{2,1,0:T(8,128)S(1)}, f32[4,64,128]{2,1,0:T(8,128)S(1)}, f32[4,64,128]{2,1,0:T(8,128)S(1)}, f32[4,64,128]{2,1,0:T(8,128)S(1)}) custom-call(s32[2]{0:T(128)S(1)} %pad_add_fusion.place_ref, f32[32,64,256]{2,1,0:T(8,128)} %rho_ref.5, bf16[4,64,256]{2,1,0:T(8,128)(2,1)} %constant.84.high_ref.sine_high_ref, ...), custom_call_target="tpu_custom_call" | custom-call | flops 1000000000 | bytes 4194304 | tf_op jit(solution)/shard_map/pallas_call | solution.py:251
  2.8 1.5 %shard_map.262 = (f32[4,64,128]{2,1,0:T(8,128)S(1)}, f32[4,64,128]{2,1,0:T(8,128)S(1)}, f32[4,64,128]{2,1,0:T(8,128)S(1)}, f32[4,64,128]{2,1,0:T(8,128)S(1)}) custom-call(s32[2]{0:T(128)S(1)} %pad_add_fusion.place_ref, f32[32,64,256]{2,1,0:T(8,128)} %rho_ref.5, bf16[4,64,256]{2,1,0:T(8,128)(2,1)} %constant.84.high_ref.sine_high_ref, ...), custom_call_target="tpu_custom_call" | custom-call | flops 1000000000 | bytes 4194304 | tf_op jit(solution)/shard_map/pallas_call | solution.py:251
  4.4 3.0 %collective-permute-start.7 = (f32[4,64,128]{2,1,0:T(8,128)S(1)}, f32[4,64,128]{2,1,0:T(8,128)S(1)}, u32[]{:S(2)}, u32[]{:S(2)}) collective-permute-start(f32[4,64,128]{2,1,0:T(8,128)S(1)} %get-tuple-element.51), channel_id=1, source_target_pairs={{0,2},{1,3},{2,0},{3,1},{4,6},{5,7},{6,4},{7,5},{8,10},{9,11},{10,... | collective-permute-start | bytes 393224 | tf_op jit(solution)/shard_map/ppermute | solution.py:357
  7.4 1.4 %collective-permute-start.1 = (f32[4,64,128]{2,1,0:T(8,128)S(1)}, f32[4,64,128]{2,1,0:T(8,128)S(1)}, u32[]{:S(2)}, u32[]{:S(2)}) collective-permute-start(f32[4,64,128]{2,1,0:T(8,128)S(1)} %get-tuple-element.42), channel_id=1, source_target_pairs={{0,2},{1,3},{2,0},{3,1},{4,6},{5,7},{6,4},{7,5},{8,10},{9,11},{10,... | collective-permute-start | bytes 393224 | tf_op jit(solution)/shard_map/ppermute | solution.py:357
  8.8 2.0 %shard_map.260 = (f32[8,64,128]{2,1,0:T(8,128)S(1)}, f32[8,64,128]{2,1,0:T(8,128)S(1)}, f32[8,64,128]{2,1,0:T(8,128)S(1)}, f32[8,64,128]{2,1,0:T(8,128)S(1)}) custom-call(s32[2]{0:T(128)S(1)} %pad_add_fusion.place_ref, f32[32,64,256]{2,1,0:T(8,128)} %rho_ref.5, bf16[4,64,256]{2,1,0:T(8,128)(2,1)} %constant.84.high_ref.sine_high_ref, ...), custom_call_target="tpu_custom_call" | custom-call | flops 1000000000 | bytes 4194304 | tf_op jit(solution)/shard_map/pallas_call | solution.py:251
  11.7 2.0 %collective-permute-start.4 = (f32[8,64,128]{2,1,0:T(8,128)S(1)}, f32[8,64,128]{2,1,0:T(8,128)S(1)}, u32[]{:S(2)}, u32[]{:S(2)}) collective-permute-start(f32[8,64,128]{2,1,0:T(8,128)S(1)} %get-tuple-element.47), channel_id=1, source_target_pairs={{0,2},{1,3},{2,0},{3,1},{4,6},{5,7},{6,4},{7,5},{8,10},{9,11},{10,... | collective-permute-start | bytes 786440 | tf_op jit(solution)/shard_map/ppermute | solution.py:357
  14.1 1.9 %collective-permute-start.5 = (f32[8,64,128]{2,1,0:T(8,128)S(1)}, f32[8,64,128]{2,1,0:T(8,128)S(1)}, u32[]{:S(2)}, u32[]{:S(2)}) collective-permute-start(f32[8,64,128]{2,1,0:T(8,128)S(1)} %get-tuple-element.48), channel_id=1, source_target_pairs={{0,3},{1,2},{2,1},{3,0},{4,7},{5,6},{6,5},{7,4},{8,11},{9,10},{10,... | collective-permute-start | bytes 786440 | tf_op jit(solution)/shard_map/ppermute | solution.py:357
  16.0 11.5 %shard_map.258 = (f32[32,64,256]{2,1,0:T(8,128)S(1)}, f32[32,64,256]{2,1,0:T(8,128)S(1)}, f32[2,3072,128]{2,1,0:T(8,128)S(1)}, f32[8,112,256]{2,1,0:T(8,128)S(1)...) custom-call(s32[2]{0:T(128)S(1)} %pad_add_fusion.place_ref, ...), custom_call_target="tpu_custom_call" | custom-call | flops 10000000000 | bytes 4194304 | tf_op jit(solution)/shard_map/pallas_call | solution.py:251
  27.6 0.6 shard_map.263.refs_2_
  28.2 0.6 shard_map.259.refs_0_
  28.9 1.3 %collective-permute-done.5.refs_3_ = f32[8,64,128]{2,1,0:T(8,128)S(1)} collective-permute-done((f32[8,64,128]{2,1,0:T(8,128)S(1)}, f32[8,64,128]{2,1,0:T(8,128)S(1)}, u32[]{:S(2)}, u32[]{:S(2)}) %collective-permute-start.5) | collective-permute-done | bytes 262176 | tf_op jit(solution)/shard_map/ppermute | solution.py:357
  30.2 1.0 shard_map.261.refs_1_
  31.4 6.4 %shard_map.264 = (f32[32,64,256]{2,1,0:T(8,128)S(1)}, f32[32,1,384]{2,1,0:T(1,128)S(1)}, f32[8,128]{1,0:T(8,128)S(1)}) custom-call(s32[2]{0:T(128)S(1)} %pad_add_fusion.place_ref, f32[17,256]{1,0:T(8,128)S(1)} %copy-done.13, f32[8,64,256]{2,1,0:T(8,128)S(1)} %shard_map.259.refs_0_, f32[16,64,256]{2,1,0:T(8,128)S(1)} %shard_map.261.refs_1_, ...), custom_call_target="tpu_custom_call" | custom-call | flops 1000000000 | bytes 4194304 | tf_op jit(solution)/shard_map/pallas_call | solution.py:251
  37.8 13.3 %all_to_all.15.share_ref = f32[32,1,384]{2,1,0:T(1,128)S(1)} all-to-all(f32[32,1,384]{2,1,0:T(1,128)S(1)} %get-tuple-element.55), channel_id=1, replica_groups=mesh['gx'=8,'gy'=4] {'gx','gy'}, dimensions={0} | all-to-all | bytes 98304 | tf_op jit(solution)/shard_map/all_to_all | solution.py:744
  51.1 5.9 %shard_map.265 = (f32[32,64,256]{2,1,0:T(8,128)S(1)}, f32[8,4,8,256]{3,2,1,0:T(8,128)S(1)}, f32[8,128]{1,0:T(8,128)S(1)}) custom-call(s32[2]{0:T(128)S(1)} %pad_add_fusion.place_ref, f32[32,1,384]{2,1,0:T(1,128)S(1)} %all_to_all.15.share_ref, f32[3,192,128]{2,1,0:T(8,128)S(1)} %get-tuple-element.56.unit_ref, bf16[256,256]{1,0:T(8,128)(2,1)S(1)} %copy-done.6, ...), custom_call_target="tpu_custom_call" | custom-call | flops 1000000000 | bytes 4194304 | tf_op jit(solution)/shard_map/pallas_call | solution.py:251
  57.0 12.1 %all_to_all.16.near_ref = f32[8,4,8,256]{3,2,1,0:T(8,128)S(1)} all-to-all(f32[8,4,8,256]{3,2,1,0:T(8,128)S(1)} %get-tuple-element.60), channel_id=1, replica_groups=mesh['gx'=8,'gy'=4] {'gx'}, dimensions={0} | all-to-all | bytes 524288 | tf_op jit(solution)/shard_map/all_to_all | solution.py:912
  69.1 0.9 shard_map.266
  70.0 11.4 %all_to_all.17.ghost_ref = f32[8,24,256]{2,1,0:T(8,128)S(1)} all-to-all(f32[8,24,256]{2,1,0:T(8,128)S(1)} %shard_map.266), channel_id=1, replica_groups=mesh['gx'=8,'gy'=4] {'gx'}, dimensions={0} | all-to-all | bytes 393216 | tf_op jit(solution)/shard_map/all_to_all | solution.py:956
  81.4 0.7 shard_map.269
  82.2 1.6 %shard_map.268 = (f32[8,64,128]{2,1,0:T(8,128)S(1)}, f32[8,64,128]{2,1,0:T(8,128)S(1)}, f32[8,64,128]{2,1,0:T(8,128)S(1)}, f32[8,64,128]{2,1,0:T(8,128)S(1)}, f32[8,256]{1,0:T(8,128)}) custom-call(f32[32,64,256]{2,1,0:T(8,128)S(1)} %get-tuple-element.58.total_ref, f32[32,64,256]{2,1,0:T(8,128)S(1)} %get-tuple-element.59.profile_ref, ...), custom_call_target="tpu_custom_call" | custom-call | flops 1000000000 | bytes 4194304 | tf_op jit(solution)/shard_map/pallas_call | solution.py:251
  84.8 0.9 collective-permute-start.14
  85.7 0.8 collective-permute-start.20
  86.5 10.9 %collective-permute-done.20.refs_9_ = f32[8,256]{1,0:T(8,128)S(1)} collective-permute-done((f32[8,256]{1,0:T(8,128)S(1)}, f32[8,256]{1,0:T(8,128)S(1)}, u32[]{:S(2)}, u32[]{:S(2)}) %collective-permute-start.20) | collective-permute-done | bytes 8224 | tf_op jit(solution)/shard_map/ppermute | solution.py:357
  97.9 1.6 %collective-permute-start.17 = (f32[4,64,128]{2,1,0:T(8,128)S(1)}, f32[4,64,128]{2,1,0:T(8,128)S(1)}, u32[]{:S(2)}, u32[]{:S(2)}) collective-permute-start(f32[4,64,128]{2,1,0:T(8,128)S(1)} %get-tuple-element.76), channel_id=1, source_target_pairs={{0,3},{1,2},{2,1},{3,0},{4,7},{5,6},{6,5},{7,4},{8,11},{9,10},{10,... | collective-permute-start | bytes 393224 | tf_op jit(solution)/shard_map/ppermute | solution.py:357
  99.5 1.1 shard_map.267
  100.6 3.1 %collective-permute-done.16.refs_2_ = f32[4,64,128]{2,1,0:T(8,128)S(1)} collective-permute-done((f32[4,64,128]{2,1,0:T(8,128)S(1)}, f32[4,64,128]{2,1,0:T(8,128)S(1)}, u32[]{:S(2)}, u32[]{:S(2)}) %collective-permute-start.16) | collective-permute-done | bytes 131104 | tf_op jit(solution)/shard_map/ppermute | solution.py:357
  103.7 2.4 %collective-permute-done.17.refs_3_ = f32[4,64,128]{2,1,0:T(8,128)S(1)} collective-permute-done((f32[4,64,128]{2,1,0:T(8,128)S(1)}, f32[4,64,128]{2,1,0:T(8,128)S(1)}, u32[]{:S(2)}, u32[]{:S(2)}) %collective-permute-start.17) | collective-permute-done | bytes 131104 | tf_op jit(solution)/shard_map/ppermute | solution.py:357
  106.6 1.0 collective-permute-start.11
  107.6 1.2 %shard_map.270.refs_5_ = f32[32,64,256]{2,1,0:T(8,128)} custom-call(f32[4,64,128]{2,1,0:T(8,128)S(1)} %get-tuple-element.73.refs_0_, f32[4,64,128]{2,1,0:T(8,128)S(1)} %collective-permute-done.15.refs_1_, f32[4,64,128]{2,1,0:T(8,128)S(1)} %collective-permute-done.16.refs_2_, f32[4,64,128]{2,1,0:T(8,128)S(1)} %collective-permute-done.17.refs_3_, ...), custom_call_target="tpu_custom_call" | custom-call | flops 1000000000 | bytes 4194304 | tf_op jit(solution)/shard_map/pallas_call | solution.py:251
  109.7 1.7 %shard_map.271.refs_5_ = f32[32,64,256]{2,1,0:T(8,128)} custom-call(f32[8,64,128]{2,1,0:T(8,128)S(1)} %get-tuple-element.69.refs_0_, f32[8,64,128]{2,1,0:T(8,128)S(1)} %collective-permute-done.12.refs_1_, f32[8,64,128]{2,1,0:T(8,128)S(1)} %collective-permute-done.13.refs_2_, ...), custom_call_target="tpu_custom_call", output_to_operand_aliasing={{}: (5, {})} | custom-call | flops 1000000000 | bytes 4194304 | tf_op jit(solution)/shard_map/pallas_call | solution.py:251
  111.3 3.3 %collective-permute-done.19.refs_8_ = f32[8,256]{1,0:T(8,128)S(1)} collective-permute-done((f32[8,256]{1,0:T(8,128)S(1)}, f32[8,256]{1,0:T(8,128)S(1)}, u32[]{:S(2)}, u32[]{:S(2)}) %collective-permute-start.19) | collective-permute-done | bytes 8224 | tf_op jit(solution)/shard_map/ppermute | solution.py:357
  114.7 1.2 %shard_map.272 = (f32[32,64,256]{2,1,0:T(8,128)}, f32[2]{0:T(128)}) custom-call(f32[4,64,128]{2,1,0:T(8,128)S(1)} %get-tuple-element.64.refs_0_, f32[4,64,128]{2,1,0:T(8,128)S(1)} %collective-permute-done.9.refs_1_, f32[4,64,128]{2,1,0:T(8,128)S(1)} %collective-permute-done.10.refs_2_, ...), custom_call_target="tpu_custom_call", output_to_operand_aliasing={{0}: (5, {})} | custom-call | flops 1000000000 | bytes 4194304 | tf_op jit(solution)/shard_map/pallas_call | solution.py:251
  (60 shorter events, 4.8 us)
Async XLA Ops:
  2.2 8.6 %collective-permute-start = (f32[4,64,128]{2,1,0:T(8,128)S(1)}, f32[4,64,128]{2,1,0:T(8,128)S(1)}, u32[]{:S(2)}, u32[]{:S(2)}) collective-permute-start(f32[4,64,128]{2,1,0:T(8,128)S(1)} %get-tuple-element.41), channel_id=1, source_target_pairs={{0,1},{1,0},{2,3},{3,2},{4,5},{5,4},{6,7},{7,6},{8,9},{9,8},{10,11... | collective-permute-start | bytes 393224 | tf_op jit(solution)/shard_map/ppermute | solution.py:357
  4.4 6.9 %collective-permute-start.6 = (f32[4,64,128]{2,1,0:T(8,128)S(1)}, f32[4,64,128]{2,1,0:T(8,128)S(1)}, u32[]{:S(2)}, u32[]{:S(2)}) collective-permute-start(f32[4,64,128]{2,1,0:T(8,128)S(1)} %get-tuple-element.50), channel_id=1, source_target_pairs={{0,1},{1,0},{2,3},{3,2},{4,5},{5,4},{6,7},{7,6},{8,9},{9,8},{10,11... | collective-permute-start | bytes 393224 | tf_op jit(solution)/shard_map/ppermute | solution.py:357
  4.4 7.3 %collective-permute-start.7 = (f32[4,64,128]{2,1,0:T(8,128)S(1)}, f32[4,64,128]{2,1,0:T(8,128)S(1)}, u32[]{:S(2)}, u32[]{:S(2)}) collective-permute-start(f32[4,64,128]{2,1,0:T(8,128)S(1)} %get-tuple-element.51), channel_id=1, source_target_pairs={{0,2},{1,3},{2,0},{3,1},{4,6},{5,7},{6,4},{7,5},{8,10},{9,11},{10,... | collective-permute-start | bytes 393224 | tf_op jit(solution)/shard_map/ppermute | solution.py:357
  7.4 6.7 %collective-permute-start.8 = (f32[4,64,128]{2,1,0:T(8,128)S(1)}, f32[4,64,128]{2,1,0:T(8,128)S(1)}, u32[]{:S(2)}, u32[]{:S(2)}) collective-permute-start(f32[4,64,128]{2,1,0:T(8,128)S(1)} %get-tuple-element.52), channel_id=1, source_target_pairs={{0,3},{1,2},{2,1},{3,0},{4,7},{5,6},{6,5},{7,4},{8,11},{9,10},{10,... | collective-permute-start | bytes 393224 | tf_op jit(solution)/shard_map/ppermute | solution.py:357
  7.4 20.8 %collective-permute-start.1 = (f32[4,64,128]{2,1,0:T(8,128)S(1)}, f32[4,64,128]{2,1,0:T(8,128)S(1)}, u32[]{:S(2)}, u32[]{:S(2)}) collective-permute-start(f32[4,64,128]{2,1,0:T(8,128)S(1)} %get-tuple-element.42), channel_id=1, source_target_pairs={{0,2},{1,3},{2,0},{3,1},{4,6},{5,7},{6,4},{7,5},{8,10},{9,11},{10,... | collective-permute-start | bytes 393224 | tf_op jit(solution)/shard_map/ppermute | solution.py:357
  10.8 17.3 %collective-permute-start.2 = (f32[4,64,128]{2,1,0:T(8,128)S(1)}, f32[4,64,128]{2,1,0:T(8,128)S(1)}, u32[]{:S(2)}, u32[]{:S(2)}) collective-permute-start(f32[4,64,128]{2,1,0:T(8,128)S(1)} %get-tuple-element.43), channel_id=1, source_target_pairs={{0,3},{1,2},{2,1},{3,0},{4,7},{5,6},{6,5},{7,4},{8,11},{9,10},{10,... | collective-permute-start | bytes 393224 | tf_op jit(solution)/shard_map/ppermute | solution.py:357
  11.2 17.7 %collective-permute-start.3 = (f32[8,64,128]{2,1,0:T(8,128)S(1)}, f32[8,64,128]{2,1,0:T(8,128)S(1)}, u32[]{:S(2)}, u32[]{:S(2)}) collective-permute-start(f32[8,64,128]{2,1,0:T(8,128)S(1)} %get-tuple-element.46), channel_id=1, source_target_pairs={{0,1},{1,0},{2,3},{3,2},{4,5},{5,4},{6,7},{7,6},{8,9},{9,8},{10,11... | collective-permute-start | bytes 786440 | tf_op jit(solution)/shard_map/ppermute | solution.py:357
  11.7 17.2 %collective-permute-start.4 = (f32[8,64,128]{2,1,0:T(8,128)S(1)}, f32[8,64,128]{2,1,0:T(8,128)S(1)}, u32[]{:S(2)}, u32[]{:S(2)}) collective-permute-start(f32[8,64,128]{2,1,0:T(8,128)S(1)} %get-tuple-element.47), channel_id=1, source_target_pairs={{0,2},{1,3},{2,0},{3,1},{4,6},{5,7},{6,4},{7,5},{8,10},{9,11},{10,... | collective-permute-start | bytes 786440 | tf_op jit(solution)/shard_map/ppermute | solution.py:357
  14.1 16.1 %collective-permute-start.5 = (f32[8,64,128]{2,1,0:T(8,128)S(1)}, f32[8,64,128]{2,1,0:T(8,128)S(1)}, u32[]{:S(2)}, u32[]{:S(2)}) collective-permute-start(f32[8,64,128]{2,1,0:T(8,128)S(1)} %get-tuple-element.48), channel_id=1, source_target_pairs={{0,3},{1,2},{2,1},{3,0},{4,7},{5,6},{6,5},{7,4},{8,11},{9,10},{10,... | collective-permute-start | bytes 786440 | tf_op jit(solution)/shard_map/ppermute | solution.py:357
  28.8 2.4 %copy-start = (f32[3,256,384]{2,1,0:T(8,128)S(1)}, f32[3,256,384]{2,1,0:T(8,128)}, u32[]{:S(2)}) copy-start(f32[3,256,384]{2,1,0:T(8,128)} %constant.78.clone.refs_11_) | copy-start | bytes 3538948
  28.8 2.4 %copy-start.2 = (bf16[2,128,256]{2,1,0:T(8,128)(2,1)S(1)}, bf16[2,128,256]{2,1,0:T(8,128)(2,1)}, u32[]{:S(2)}) copy-start(bf16[2,128,256]{2,1,0:T(8,128)(2,1)} %constant.86.refs_9_) | copy-start | bytes 393220
  28.8 2.4 %copy-start.7 = (bf16[256,128]{1,0:T(8,128)(2,1)S(1)}, bf16[256,128]{1,0:T(8,128)(2,1)}, u32[]{:S(2)}) copy-start(bf16[256,128]{1,0:T(8,128)(2,1)} %constant.73.clone.refs_6_) | copy-start | bytes 196612
  28.8 2.4 %copy-start.8 = (bf16[256,128]{1,0:T(8,128)(2,1)S(1)}, bf16[256,128]{1,0:T(8,128)(2,1)}, u32[]{:S(2)}) copy-start(bf16[256,128]{1,0:T(8,128)(2,1)} %constant.72.clone.refs_5_) | copy-start | bytes 196612
  28.8 2.4 %copy-start.9 = (f32[2,24,256]{2,1,0:T(8,128)S(1)}, f32[2,24,256]{2,1,0:T(8,128)}, u32[]{:S(2)}) copy-start(f32[2,24,256]{2,1,0:T(8,128)} %constant.77.clone.refs_10_) | copy-start | bytes 147460
  31.3 19.8 %copy-start.1 = (f32[2,256,128]{2,1,0:T(8,128)S(1)}, f32[2,256,128]{2,1,0:T(8,128)}, u32[]{:S(2)}) copy-start(f32[2,256,128]{2,1,0:T(8,128)} %constant.71.clone.column_ref) | copy-start | bytes 786436
  31.3 19.8 %copy-start.3 = (bf16[4,64,256]{2,1,0:T(8,128)(2,1)S(1)}, bf16[4,64,256]{2,1,0:T(8,128)(2,1)}, u32[]{:S(2)}) copy-start(bf16[4,64,256]{2,1,0:T(8,128)(2,1)} %constant.83.clone.local_low_ref) | copy-start | bytes 393220
  31.3 19.8 %copy-start.4 = (bf16[4,64,256]{2,1,0:T(8,128)(2,1)S(1)}, bf16[4,64,256]{2,1,0:T(8,128)(2,1)}, u32[]{:S(2)}) copy-start(bf16[4,64,256]{2,1,0:T(8,128)(2,1)} %constant.82.clone.local_high_ref) | copy-start | bytes 393220
  31.3 19.8 %copy-start.5 = (bf16[256,256]{1,0:T(8,128)(2,1)S(1)}, bf16[256,256]{1,0:T(8,128)(2,1)}, u32[]{:S(2)}) copy-start(bf16[256,256]{1,0:T(8,128)(2,1)} %constant.81.clone.folded_low_ref) | copy-start | bytes 393220
  31.3 19.8 %copy-start.6 = (bf16[256,256]{1,0:T(8,128)(2,1)S(1)}, bf16[256,256]{1,0:T(8,128)(2,1)}, u32[]{:S(2)}) copy-start(bf16[256,256]{1,0:T(8,128)(2,1)} %constant.80.clone.folded_high_ref) | copy-start | bytes 393220
  31.4 19.8 %copy-start.14 = (f32[8,256]{1,0:T(8,128)S(1)}, f32[8,256]{1,0:T(8,128)}, u32[]{:S(2)}) copy-start(f32[8,256]{1,0:T(8,128)} %constant.70.clone.row_ref) | copy-start | bytes 24580
  82.1 15.8 %collective-permute-start.15 = (f32[4,64,128]{2,1,0:T(8,128)S(1)}, f32[4,64,128]{2,1,0:T(8,128)S(1)}, u32[]{:S(2)}, u32[]{:S(2)}) collective-permute-start(f32[4,64,128]{2,1,0:T(8,128)S(1)} %get-tuple-element.74), channel_id=1, source_target_pairs={{0,1},{1,0},{2,3},{3,2},{4,5},{5,4},{6,7},{7,6},{8,9},{9,8},{10,11... | collective-permute-start | bytes 393224 | tf_op jit(solution)/shard_map/ppermute | solution.py:357
  83.8 22.8 %collective-permute-start.12 = (f32[8,64,128]{2,1,0:T(8,128)S(1)}, f32[8,64,128]{2,1,0:T(8,128)S(1)}, u32[]{:S(2)}, u32[]{:S(2)}) collective-permute-start(f32[8,64,128]{2,1,0:T(8,128)S(1)} %get-tuple-element.70), channel_id=1, source_target_pairs={{0,1},{1,0},{2,3},{3,2},{4,5},{5,4},{6,7},{7,6},{8,9},{9,8},{10,11... | collective-permute-start | bytes 786440 | tf_op jit(solution)/shard_map/ppermute | solution.py:357
  84.3 24.6 %collective-permute-start.13 = (f32[8,64,128]{2,1,0:T(8,128)S(1)}, f32[8,64,128]{2,1,0:T(8,128)S(1)}, u32[]{:S(2)}, u32[]{:S(2)}) collective-permute-start(f32[8,64,128]{2,1,0:T(8,128)S(1)} %get-tuple-element.71), channel_id=1, source_target_pairs={{0,2},{1,3},{2,0},{3,1},{4,6},{5,7},{6,4},{7,5},{8,10},{9,11},{10,... | collective-permute-start | bytes 786440 | tf_op jit(solution)/shard_map/ppermute | solution.py:357
  84.8 24.7 %collective-permute-start.14 = (f32[8,64,128]{2,1,0:T(8,128)S(1)}, f32[8,64,128]{2,1,0:T(8,128)S(1)}, u32[]{:S(2)}, u32[]{:S(2)}) collective-permute-start(f32[8,64,128]{2,1,0:T(8,128)S(1)} %get-tuple-element.72), channel_id=1, source_target_pairs={{0,3},{1,2},{2,1},{3,0},{4,7},{5,6},{6,5},{7,4},{8,11},{9,10},{10,... | collective-permute-start | bytes 786440 | tf_op jit(solution)/shard_map/ppermute | solution.py:357
  85.7 11.7 %collective-permute-start.20 = (f32[8,256]{1,0:T(8,128)S(1)}, f32[8,256]{1,0:T(8,128)S(1)}, u32[]{:S(2)}, u32[]{:S(2)}) collective-permute-start(f32[8,256]{1,0:T(8,128)S(1)} %get-tuple-element.77.refs_6_), channel_id=1, source_target_pairs={{0,3},{1,2},{2,1},{3,0},{4,7},{5,6},{6,5},{7,4},{8,11},{9,10},{10,... | collective-permute-start | bytes 24584 | tf_op jit(solution)/shard_map/ppermute | solution.py:357
  97.4 6.4 %collective-permute-start.16 = (f32[4,64,128]{2,1,0:T(8,128)S(1)}, f32[4,64,128]{2,1,0:T(8,128)S(1)}, u32[]{:S(2)}, u32[]{:S(2)}) collective-permute-start(f32[4,64,128]{2,1,0:T(8,128)S(1)} %get-tuple-element.75), channel_id=1, source_target_pairs={{0,2},{1,3},{2,0},{3,1},{4,6},{5,7},{6,4},{7,5},{8,10},{9,11},{10,... | collective-permute-start | bytes 393224 | tf_op jit(solution)/shard_map/ppermute | solution.py:357
  97.9 8.3 %collective-permute-start.17 = (f32[4,64,128]{2,1,0:T(8,128)S(1)}, f32[4,64,128]{2,1,0:T(8,128)S(1)}, u32[]{:S(2)}, u32[]{:S(2)}) collective-permute-start(f32[4,64,128]{2,1,0:T(8,128)S(1)} %get-tuple-element.76), channel_id=1, source_target_pairs={{0,3},{1,2},{2,1},{3,0},{4,7},{5,6},{6,5},{7,4},{8,11},{9,10},{10,... | collective-permute-start | bytes 393224 | tf_op jit(solution)/shard_map/ppermute | solution.py:357
  103.7 10.9 %collective-permute-start.9 = (f32[4,64,128]{2,1,0:T(8,128)S(1)}, f32[4,64,128]{2,1,0:T(8,128)S(1)}, u32[]{:S(2)}, u32[]{:S(2)}) collective-permute-start(f32[4,64,128]{2,1,0:T(8,128)S(1)} %get-tuple-element.65), channel_id=1, source_target_pairs={{0,1},{1,0},{2,3},{3,2},{4,5},{5,4},{6,7},{7,6},{8,9},{9,8},{10,11... | collective-permute-start | bytes 393224 | tf_op jit(solution)/shard_map/ppermute | solution.py:357
  106.2 8.5 %collective-permute-start.10 = (f32[4,64,128]{2,1,0:T(8,128)S(1)}, f32[4,64,128]{2,1,0:T(8,128)S(1)}, u32[]{:S(2)}, u32[]{:S(2)}) collective-permute-start(f32[4,64,128]{2,1,0:T(8,128)S(1)} %get-tuple-element.66), channel_id=1, source_target_pairs={{0,2},{1,3},{2,0},{3,1},{4,6},{5,7},{6,4},{7,5},{8,10},{9,11},{10,... | collective-permute-start | bytes 393224 | tf_op jit(solution)/shard_map/ppermute | solution.py:357
  106.6 8.1 %collective-permute-start.11 = (f32[4,64,128]{2,1,0:T(8,128)S(1)}, f32[4,64,128]{2,1,0:T(8,128)S(1)}, u32[]{:S(2)}, u32[]{:S(2)}) collective-permute-start(f32[4,64,128]{2,1,0:T(8,128)S(1)} %get-tuple-element.67), channel_id=1, source_target_pairs={{0,3},{1,2},{2,1},{3,0},{4,7},{5,6},{6,5},{7,4},{8,11},{9,10},{10,... | collective-permute-start | bytes 393224 | tf_op jit(solution)/shard_map/ppermute | solution.py:357
  108.8 5.8 %collective-permute-start.19 = (f32[8,256]{1,0:T(8,128)S(1)}, f32[8,256]{1,0:T(8,128)S(1)}, u32[]{:S(2)}, u32[]{:S(2)}) collective-permute-start(f32[8,256]{1,0:T(8,128)S(1)} %get-tuple-element.77.refs_6_), channel_id=1, source_target_pairs={{0,2},{1,3},{2,0},{3,1},{4,6},{5,7},{6,4},{7,5},{8,10},{9,11},{10,... | collective-permute-start | bytes 24584 | tf_op jit(solution)/shard_map/ppermute | solution.py:357
  109.4 5.2 %collective-permute-start.18 = (f32[8,256]{1,0:T(8,128)S(1)}, f32[8,256]{1,0:T(8,128)S(1)}, u32[]{:S(2)}, u32[]{:S(2)}) collective-permute-start(f32[8,256]{1,0:T(8,128)S(1)} %get-tuple-element.77.refs_6_), channel_id=1, source_target_pairs={{0,1},{1,0},{2,3},{3,2},{4,5},{5,4},{6,7},{7,6},{8,9},{9,8},{10,11... | collective-permute-start | bytes 24584 | tf_op jit(solution)/shard_map/ppermute | solution.py:357
  (4 other events, 9.6 us)

commit v2 on v1

--- a/solution.py
+++ b/solution.py
@@ -13,7 +13,7 @@
 COUNT = ORDER + 1
 PAIRS = 256
 NEWTON = 1
-FACE_ROWS = 16
+FACE_ROWS = 8
 TERMS = 384
 outer_ratio = 1.1
 radius_scale = math.sqrt(3.0) / 2.0
@@ -408,6 +408,7 @@
         unit_ref,
         pair_ref,
         table_ref,
+        legendre_ref,
         values,
         probe_high,
         probe_low,
@@ -471,6 +472,14 @@
         here = pl.ds(pl.multiple_of(index_x * cells_a, cells_a), cells_a)
         middle = jnp.full((8, half), 0.5, F32)[0:1]
         along = cell_row_ref[0:1, :]
+        point = 2.0 * cell_column_ref[here, :]
+        older, newer = jnp.ones_like(point), point
+        legendre_ref[0] = older
+        for degree in range(1, COUNT):
+            legendre_ref[degree] = newer
+            older, newer = newer, (
+                (2 * degree + 1) / (degree + 1) * point * newer - degree / (degree + 1) * older
+            )
         for begin, count, first, second, third in (
             (0, cells_a, cell_column_ref[here, :], middle, along),
             (cells_a, cells_a, cell_column_ref[here, :], along, middle),
@@ -504,7 +513,7 @@
         prepare_body,
         (1,),
         [SCALARS] + [block_of(array) for array in inputs],
-        [RESIDENT] * 7,
+        [RESIDENT] * 8,
         [
             field,
             field,
@@ -513,6 +522,7 @@
             kept(3, 2 * cells_a + half, half),
             pltpu.VMEM((2, groups_y * lanes, wide), BF16),
             pltpu.VMEM((2, length, length), BF16),
+            kept(COUNT, cells_a, half),
         ],
         [
             pltpu.VMEM((depth, length), F32),
@@ -522,7 +532,6 @@
         10**10,
         limit=pair_limit,
     )(place, *inputs)
-    legendre = put(tabs["legendre"])
     edge_rows = put(np.concatenate([tabs["edges"], np.zeros((6, length))]))
     edge_columns = put(np.broadcast_to(tabs["edges"][:, :, None], (2, length, 128)))
     column_high, column_low = (jnp.asarray(t) for t in split_np(tabs["columns"]))
@@ -533,7 +542,7 @@
     lookup = lookup.reshape(groups_y, 24, blocks, block).transpose(0, 2, 1, 3)
     lookup_high, lookup_low = (jnp.asarray(t) for t in split_np(lookup))
     spread = jnp.asarray(tabs["spread"].astype(np.float32)).astype(BF16)
-    factors, profile, probe_table, green_table, units, pairs, table = tables
+    factors, profile, probe_table, green_table, units, pairs, table, legendre = tables
 
     def second_body(*refs):
         blocks_in = refs[:groups_y]
@@ -569,7 +578,7 @@
             )(*parts, pairs)
         )
 
-    rows_now = min(32, block)
+    rows_now = min(64, block)
 
     def solve_body(place_ref, leg_ref, *refs):
         given = refs[: len(going)]
@@ -641,7 +650,7 @@
                 )
             return outs
 
-        many_rows = min(16, cells_a)
+        many_rows = min(32, cells_a)
         for start in range(0, cells_a, many_rows):
             stack = field_ref[start : start + many_rows, window, :].reshape(
                 many_rows * block, length
@@ -650,7 +659,7 @@
             for item in range(COUNT):
                 value = tensor[item]
                 for inner, out in enumerate(outs):
-                    value = value + leg_ref[item, index_x * cells_a + start + inner] * out
+                    value = value + leg_ref[item, start + inner : start + inner + 1, 0:128] * out
                 tensor[item] = value
             if start == 0:
                 tensor[COUNT] += begin * outs[0]
@@ -665,7 +674,7 @@
                 [probe_ref[part, rows, :] for part in range(length // 128)], axis=1
             )
 
-        group = 10
+        group = 19
         for start in range(0, functions, group):
             items = range(start, min(start + group, functions))
             stack = jnp.concatenate(
@@ -719,7 +728,7 @@
     solved, moments, energy_one = call(
         solve_body,
         (blocks,),
-        [SCALARS] * 2 + [RESIDENT] * (len(going) + 10),
+        [SCALARS] + [RESIDENT] * (len(going) + 11),
         [RESIDENT] * 3,
         [field, kept(devices, 1, TERMS), kept(8, 128)],
         [

time: 116 us -> 116 us (level)
  no operation moved by 1% of the time
where the time goes in v2:
time: 116 us
  Pallas kernels  39.2 us (34%)
  blocking collectives  36.6 us (32%)
  waiting for transfers between devices  21.5 us (19%)
  starting transfers between devices  16.9 us (15%)
    pallas_call x16, Pallas kernels, run(): return kernel(*placed)  39.2 us
    ppermute x21, waiting for transfers between devices, exchange(): received.append(lax.ppermute(parts[shift], 'gy', ring))  21.5 us
    ppermute x21, starting transfers between devices, exchange(): received.append(lax.ppermute(parts[shift], 'gy', ring))  16.9 us
    all_to_all x1, blocking collectives, shards(): shared = lax.all_to_all(moments, ('gx', 'gy'), 0, 0, tiled=True)  13.3 us
    all_to_all x1, blocking collectives, shards(): gathered = lax.all_to_all(nears, 'gx', 0, 0, tiled=True)  11.9 us
    all_to_all x1, blocking collectives, shards(): returned = lax.all_to_all(answers, 'gx', 0, 0, tiled=True)  11.4 us
  transfers between devices with their start and end apart: 21, of which 7 were waited for; matrix products, arithmetic and copies ran while one was open for 0% of the time, Pallas kernels for 19%

profile of v2, /device:TPU:0, one launch (start us, length us, event | category | flops | bytes accessed | tf_op | source)
XLA Modules:
  0.0 115.6 jit_solution(7178499843987997948)
XLA Ops:
  0.7 1.5 %shard_map.249 = (f32[4,64,128]{2,1,0:T(8,128)S(1)}, f32[4,64,128]{2,1,0:T(8,128)S(1)}, f32[4,64,128]{2,1,0:T(8,128)S(1)}, f32[4,64,128]{2,1,0:T(8,128)S(1)}) custom-call(s32[2]{0:T(128)S(1)} %pad_add_fusion.place_ref, f32[32,64,256]{2,1,0:T(8,128)} %rho_ref.5, bf16[4,64,256]{2,1,0:T(8,128)(2,1)} %constant.81.sine_high_ref.high_ref, ...), custom_call_target="tpu_custom_call" | custom-call | flops 1000000000 | bytes 4194304 | tf_op jit(solution)/shard_map/pallas_call | solution.py:251
  2.8 1.5 %shard_map.253 = (f32[4,64,128]{2,1,0:T(8,128)S(1)}, f32[4,64,128]{2,1,0:T(8,128)S(1)}, f32[4,64,128]{2,1,0:T(8,128)S(1)}, f32[4,64,128]{2,1,0:T(8,128)S(1)}) custom-call(s32[2]{0:T(128)S(1)} %pad_add_fusion.place_ref, f32[32,64,256]{2,1,0:T(8,128)} %rho_ref.5, bf16[4,64,256]{2,1,0:T(8,128)(2,1)} %constant.81.sine_high_ref.high_ref, ...), custom_call_target="tpu_custom_call" | custom-call | flops 1000000000 | bytes 4194304 | tf_op jit(solution)/shard_map/pallas_call | solution.py:251
  4.4 3.0 %collective-permute-start.7 = (f32[4,64,128]{2,1,0:T(8,128)S(1)}, f32[4,64,128]{2,1,0:T(8,128)S(1)}, u32[]{:S(2)}, u32[]{:S(2)}) collective-permute-start(f32[4,64,128]{2,1,0:T(8,128)S(1)} %get-tuple-element.53), channel_id=1, source_target_pairs={{0,2},{1,3},{2,0},{3,1},{4,6},{5,7},{6,4},{7,5},{8,10},{9,11},{10,... | collective-permute-start | bytes 393224 | tf_op jit(solution)/shard_map/ppermute | solution.py:357
  7.4 1.4 %collective-permute-start.1 = (f32[4,64,128]{2,1,0:T(8,128)S(1)}, f32[4,64,128]{2,1,0:T(8,128)S(1)}, u32[]{:S(2)}, u32[]{:S(2)}) collective-permute-start(f32[4,64,128]{2,1,0:T(8,128)S(1)} %get-tuple-element.44), channel_id=1, source_target_pairs={{0,2},{1,3},{2,0},{3,1},{4,6},{5,7},{6,4},{7,5},{8,10},{9,11},{10,... | collective-permute-start | bytes 393224 | tf_op jit(solution)/shard_map/ppermute | solution.py:357
  8.8 2.0 %shard_map.251 = (f32[8,64,128]{2,1,0:T(8,128)S(1)}, f32[8,64,128]{2,1,0:T(8,128)S(1)}, f32[8,64,128]{2,1,0:T(8,128)S(1)}, f32[8,64,128]{2,1,0:T(8,128)S(1)}) custom-call(s32[2]{0:T(128)S(1)} %pad_add_fusion.place_ref, f32[32,64,256]{2,1,0:T(8,128)} %rho_ref.5, bf16[4,64,256]{2,1,0:T(8,128)(2,1)} %constant.81.sine_high_ref.high_ref, ...), custom_call_target="tpu_custom_call" | custom-call | flops 1000000000 | bytes 4194304 | tf_op jit(solution)/shard_map/pallas_call | solution.py:251
  11.7 2.0 %collective-permute-start.4 = (f32[8,64,128]{2,1,0:T(8,128)S(1)}, f32[8,64,128]{2,1,0:T(8,128)S(1)}, u32[]{:S(2)}, u32[]{:S(2)}) collective-permute-start(f32[8,64,128]{2,1,0:T(8,128)S(1)} %get-tuple-element.49), channel_id=1, source_target_pairs={{0,2},{1,3},{2,0},{3,1},{4,6},{5,7},{6,4},{7,5},{8,10},{9,11},{10,... | collective-permute-start | bytes 786440 | tf_op jit(solution)/shard_map/ppermute | solution.py:357
  14.1 1.9 %collective-permute-start.5 = (f32[8,64,128]{2,1,0:T(8,128)S(1)}, f32[8,64,128]{2,1,0:T(8,128)S(1)}, u32[]{:S(2)}, u32[]{:S(2)}) collective-permute-start(f32[8,64,128]{2,1,0:T(8,128)S(1)} %get-tuple-element.50), channel_id=1, source_target_pairs={{0,3},{1,2},{2,1},{3,0},{4,7},{5,6},{6,5},{7,4},{8,11},{9,10},{10,... | collective-permute-start | bytes 786440 | tf_op jit(solution)/shard_map/ppermute | solution.py:357
  16.0 11.6 %shard_map.248 = (f32[32,64,256]{2,1,0:T(8,128)S(1)}, f32[32,64,256]{2,1,0:T(8,128)S(1)}, f32[2,3072,128]{2,1,0:T(8,128)S(1)}, f32[8,112,256]{2,1,0:T(8,128)S(1)...) custom-call(s32[2]{0:T(128)S(1)} %pad_add_fusion.place_ref, ...), custom_call_target="tpu_custom_call" | custom-call | flops 10000000000 | bytes 4194304 | tf_op jit(solution)/shard_map/pallas_call | solution.py:251
  27.6 0.6 shard_map.254.refs_2_
  28.2 0.6 shard_map.250.refs_0_
  28.9 1.3 %collective-permute-done.5.refs_3_ = f32[8,64,128]{2,1,0:T(8,128)S(1)} collective-permute-done((f32[8,64,128]{2,1,0:T(8,128)S(1)}, f32[8,64,128]{2,1,0:T(8,128)S(1)}, u32[]{:S(2)}, u32[]{:S(2)}) %collective-permute-start.5) | collective-permute-done | bytes 262176 | tf_op jit(solution)/shard_map/ppermute | solution.py:357
  30.2 1.0 shard_map.252.refs_1_
  31.3 6.1 %shard_map.255 = (f32[32,64,256]{2,1,0:T(8,128)S(1)}, f32[32,1,384]{2,1,0:T(1,128)S(1)}, f32[8,128]{1,0:T(8,128)S(1)}) custom-call(s32[2]{0:T(128)S(1)} %pad_add_fusion.place_ref, f32[17,32,128]{2,1,0:T(8,128)S(1)} %get-tuple-element.41.leg_ref, f32[8,64,256]{2,1,0:T(8,128)S(1)} %shard_map.250.refs_0_, f32[16,64,256]{2,1,0:T(8,128)S(1)} %shard_map.252.refs_1_, ...), custom_call_target="tpu_custom_call" | custom-call | flops 1000000000 | bytes 4194304 | tf_op jit(solution)/shard_map/pallas_call | solution.py:251
  37.5 13.3 %all_to_all.15.share_ref = f32[32,1,384]{2,1,0:T(1,128)S(1)} all-to-all(f32[32,1,384]{2,1,0:T(1,128)S(1)} %get-tuple-element.57), channel_id=1, replica_groups=mesh['gx'=8,'gy'=4] {'gx','gy'}, dimensions={0} | all-to-all | bytes 98304 | tf_op jit(solution)/shard_map/all_to_all | solution.py:753
  50.8 5.9 %shard_map.256 = (f32[32,64,256]{2,1,0:T(8,128)S(1)}, f32[8,4,8,256]{3,2,1,0:T(8,128)S(1)}, f32[8,128]{1,0:T(8,128)S(1)}) custom-call(s32[2]{0:T(128)S(1)} %pad_add_fusion.place_ref, f32[32,1,384]{2,1,0:T(1,128)S(1)} %all_to_all.15.share_ref, f32[3,192,128]{2,1,0:T(8,128)S(1)} %get-tuple-element.58.unit_ref, bf16[256,256]{1,0:T(8,128)(2,1)S(1)} %copy-done.6, ...), custom_call_target="tpu_custom_call" | custom-call | flops 1000000000 | bytes 4194304 | tf_op jit(solution)/shard_map/pallas_call | solution.py:251
  56.7 11.9 %all_to_all.16.near_ref = f32[8,4,8,256]{3,2,1,0:T(8,128)S(1)} all-to-all(f32[8,4,8,256]{3,2,1,0:T(8,128)S(1)} %get-tuple-element.62), channel_id=1, replica_groups=mesh['gx'=8,'gy'=4] {'gx'}, dimensions={0} | all-to-all | bytes 524288 | tf_op jit(solution)/shard_map/all_to_all | solution.py:921
  68.6 0.9 shard_map.257
  69.5 11.4 %all_to_all.17.ghost_ref = f32[8,24,256]{2,1,0:T(8,128)S(1)} all-to-all(f32[8,24,256]{2,1,0:T(8,128)S(1)} %shard_map.257), channel_id=1, replica_groups=mesh['gx'=8,'gy'=4] {'gx'}, dimensions={0} | all-to-all | bytes 393216 | tf_op jit(solution)/shard_map/all_to_all | solution.py:965
  81.0 0.7 shard_map.260
  81.7 1.6 %shard_map.259 = (f32[8,64,128]{2,1,0:T(8,128)S(1)}, f32[8,64,128]{2,1,0:T(8,128)S(1)}, f32[8,64,128]{2,1,0:T(8,128)S(1)}, f32[8,64,128]{2,1,0:T(8,128)S(1)}, f32[8,256]{1,0:T(8,128)}) custom-call(f32[32,64,256]{2,1,0:T(8,128)S(1)} %get-tuple-element.60.total_ref, f32[32,64,256]{2,1,0:T(8,128)S(1)} %get-tuple-element.61.profile_ref, ...), custom_call_target="tpu_custom_call" | custom-call | flops 1000000000 | bytes 4194304 | tf_op jit(solution)/shard_map/pallas_call | solution.py:251
  84.3 0.9 collective-permute-start.14
  85.2 0.8 collective-permute-start.20
  86.0 10.9 %collective-permute-done.20.refs_9_ = f32[8,256]{1,0:T(8,128)S(1)} collective-permute-done((f32[8,256]{1,0:T(8,128)S(1)}, f32[8,256]{1,0:T(8,128)S(1)}, u32[]{:S(2)}, u32[]{:S(2)}) %collective-permute-start.20) | collective-permute-done | bytes 8224 | tf_op jit(solution)/shard_map/ppermute | solution.py:357
  97.4 1.6 %collective-permute-start.17 = (f32[4,64,128]{2,1,0:T(8,128)S(1)}, f32[4,64,128]{2,1,0:T(8,128)S(1)}, u32[]{:S(2)}, u32[]{:S(2)}) collective-permute-start(f32[4,64,128]{2,1,0:T(8,128)S(1)} %get-tuple-element.78), channel_id=1, source_target_pairs={{0,3},{1,2},{2,1},{3,0},{4,7},{5,6},{6,5},{7,4},{8,11},{9,10},{10,... | collective-permute-start | bytes 393224 | tf_op jit(solution)/shard_map/ppermute | solution.py:357
  99.0 1.1 shard_map.258
  100.1 3.1 %collective-permute-done.16.refs_2_ = f32[4,64,128]{2,1,0:T(8,128)S(1)} collective-permute-done((f32[4,64,128]{2,1,0:T(8,128)S(1)}, f32[4,64,128]{2,1,0:T(8,128)S(1)}, u32[]{:S(2)}, u32[]{:S(2)}) %collective-permute-start.16) | collective-permute-done | bytes 131104 | tf_op jit(solution)/shard_map/ppermute | solution.py:357
  103.2 2.4 %collective-permute-done.17.refs_3_ = f32[4,64,128]{2,1,0:T(8,128)S(1)} collective-permute-done((f32[4,64,128]{2,1,0:T(8,128)S(1)}, f32[4,64,128]{2,1,0:T(8,128)S(1)}, u32[]{:S(2)}, u32[]{:S(2)}) %collective-permute-start.17) | collective-permute-done | bytes 131104 | tf_op jit(solution)/shard_map/ppermute | solution.py:357
  106.1 1.0 collective-permute-start.11
  107.1 1.2 %shard_map.261.refs_5_ = f32[32,64,256]{2,1,0:T(8,128)} custom-call(f32[4,64,128]{2,1,0:T(8,128)S(1)} %get-tuple-element.75.refs_0_, f32[4,64,128]{2,1,0:T(8,128)S(1)} %collective-permute-done.15.refs_1_, f32[4,64,128]{2,1,0:T(8,128)S(1)} %collective-permute-done.16.refs_2_, f32[4,64,128]{2,1,0:T(8,128)S(1)} %collective-permute-done.17.refs_3_, ...), custom_call_target="tpu_custom_call" | custom-call | flops 1000000000 | bytes 4194304 | tf_op jit(solution)/shard_map/pallas_call | solution.py:251
  109.2 1.6 %shard_map.262.refs_5_ = f32[32,64,256]{2,1,0:T(8,128)} custom-call(f32[8,64,128]{2,1,0:T(8,128)S(1)} %get-tuple-element.71.refs_0_, f32[8,64,128]{2,1,0:T(8,128)S(1)} %collective-permute-done.12.refs_1_, f32[8,64,128]{2,1,0:T(8,128)S(1)} %collective-permute-done.13.refs_2_, ...), custom_call_target="tpu_custom_call", output_to_operand_aliasing={{}: (5, {})} | custom-call | flops 1000000000 | bytes 4194304 | tf_op jit(solution)/shard_map/pallas_call | solution.py:251
  110.8 3.3 %collective-permute-done.19.refs_8_ = f32[8,256]{1,0:T(8,128)S(1)} collective-permute-done((f32[8,256]{1,0:T(8,128)S(1)}, f32[8,256]{1,0:T(8,128)S(1)}, u32[]{:S(2)}, u32[]{:S(2)}) %collective-permute-start.19) | collective-permute-done | bytes 8224 | tf_op jit(solution)/shard_map/ppermute | solution.py:357
  114.2 1.2 %shard_map.263 = (f32[32,64,256]{2,1,0:T(8,128)}, f32[2]{0:T(128)}) custom-call(f32[4,64,128]{2,1,0:T(8,128)S(1)} %get-tuple-element.66.refs_0_, f32[4,64,128]{2,1,0:T(8,128)S(1)} %collective-permute-done.9.refs_1_, f32[4,64,128]{2,1,0:T(8,128)S(1)} %collective-permute-done.10.refs_2_, ...), custom_call_target="tpu_custom_call", output_to_operand_aliasing={{0}: (5, {})} | custom-call | flops 1000000000 | bytes 4194304 | tf_op jit(solution)/shard_map/pallas_call | solution.py:251
  (58 shorter events, 4.9 us)
Async XLA Ops:
  2.2 8.6 %collective-permute-start = (f32[4,64,128]{2,1,0:T(8,128)S(1)}, f32[4,64,128]{2,1,0:T(8,128)S(1)}, u32[]{:S(2)}, u32[]{:S(2)}) collective-permute-start(f32[4,64,128]{2,1,0:T(8,128)S(1)} %get-tuple-element.43), channel_id=1, source_target_pairs={{0,1},{1,0},{2,3},{3,2},{4,5},{5,4},{6,7},{7,6},{8,9},{9,8},{10,11... | collective-permute-start | bytes 393224 | tf_op jit(solution)/shard_map/ppermute | solution.py:357
  4.4 6.9 %collective-permute-start.6 = (f32[4,64,128]{2,1,0:T(8,128)S(1)}, f32[4,64,128]{2,1,0:T(8,128)S(1)}, u32[]{:S(2)}, u32[]{:S(2)}) collective-permute-start(f32[4,64,128]{2,1,0:T(8,128)S(1)} %get-tuple-element.52), channel_id=1, source_target_pairs={{0,1},{1,0},{2,3},{3,2},{4,5},{5,4},{6,7},{7,6},{8,9},{9,8},{10,11... | collective-permute-start | bytes 393224 | tf_op jit(solution)/shard_map/ppermute | solution.py:357
  4.4 7.3 %collective-permute-start.7 = (f32[4,64,128]{2,1,0:T(8,128)S(1)}, f32[4,64,128]{2,1,0:T(8,128)S(1)}, u32[]{:S(2)}, u32[]{:S(2)}) collective-permute-start(f32[4,64,128]{2,1,0:T(8,128)S(1)} %get-tuple-element.53), channel_id=1, source_target_pairs={{0,2},{1,3},{2,0},{3,1},{4,6},{5,7},{6,4},{7,5},{8,10},{9,11},{10,... | collective-permute-start | bytes 393224 | tf_op jit(solution)/shard_map/ppermute | solution.py:357
  7.4 6.7 %collective-permute-start.8 = (f32[4,64,128]{2,1,0:T(8,128)S(1)}, f32[4,64,128]{2,1,0:T(8,128)S(1)}, u32[]{:S(2)}, u32[]{:S(2)}) collective-permute-start(f32[4,64,128]{2,1,0:T(8,128)S(1)} %get-tuple-element.54), channel_id=1, source_target_pairs={{0,3},{1,2},{2,1},{3,0},{4,7},{5,6},{6,5},{7,4},{8,11},{9,10},{10,... | collective-permute-start | bytes 393224 | tf_op jit(solution)/shard_map/ppermute | solution.py:357
  7.4 20.8 %collective-permute-start.1 = (f32[4,64,128]{2,1,0:T(8,128)S(1)}, f32[4,64,128]{2,1,0:T(8,128)S(1)}, u32[]{:S(2)}, u32[]{:S(2)}) collective-permute-start(f32[4,64,128]{2,1,0:T(8,128)S(1)} %get-tuple-element.44), channel_id=1, source_target_pairs={{0,2},{1,3},{2,0},{3,1},{4,6},{5,7},{6,4},{7,5},{8,10},{9,11},{10,... | collective-permute-start | bytes 393224 | tf_op jit(solution)/shard_map/ppermute | solution.py:357
  10.8 17.3 %collective-permute-start.2 = (f32[4,64,128]{2,1,0:T(8,128)S(1)}, f32[4,64,128]{2,1,0:T(8,128)S(1)}, u32[]{:S(2)}, u32[]{:S(2)}) collective-permute-start(f32[4,64,128]{2,1,0:T(8,128)S(1)} %get-tuple-element.45), channel_id=1, source_target_pairs={{0,3},{1,2},{2,1},{3,0},{4,7},{5,6},{6,5},{7,4},{8,11},{9,10},{10,... | collective-permute-start | bytes 393224 | tf_op jit(solution)/shard_map/ppermute | solution.py:357
  11.2 17.7 %collective-permute-start.3 = (f32[8,64,128]{2,1,0:T(8,128)S(1)}, f32[8,64,128]{2,1,0:T(8,128)S(1)}, u32[]{:S(2)}, u32[]{:S(2)}) collective-permute-start(f32[8,64,128]{2,1,0:T(8,128)S(1)} %get-tuple-element.48), channel_id=1, source_target_pairs={{0,1},{1,0},{2,3},{3,2},{4,5},{5,4},{6,7},{7,6},{8,9},{9,8},{10,11... | collective-permute-start | bytes 786440 | tf_op jit(solution)/shard_map/ppermute | solution.py:357
  11.7 17.2 %collective-permute-start.4 = (f32[8,64,128]{2,1,0:T(8,128)S(1)}, f32[8,64,128]{2,1,0:T(8,128)S(1)}, u32[]{:S(2)}, u32[]{:S(2)}) collective-permute-start(f32[8,64,128]{2,1,0:T(8,128)S(1)} %get-tuple-element.49), channel_id=1, source_target_pairs={{0,2},{1,3},{2,0},{3,1},{4,6},{5,7},{6,4},{7,5},{8,10},{9,11},{10,... | collective-permute-start | bytes 786440 | tf_op jit(solution)/shard_map/ppermute | solution.py:357
  14.1 16.1 %collective-permute-start.5 = (f32[8,64,128]{2,1,0:T(8,128)S(1)}, f32[8,64,128]{2,1,0:T(8,128)S(1)}, u32[]{:S(2)}, u32[]{:S(2)}) collective-permute-start(f32[8,64,128]{2,1,0:T(8,128)S(1)} %get-tuple-element.50), channel_id=1, source_target_pairs={{0,3},{1,2},{2,1},{3,0},{4,7},{5,6},{6,5},{7,4},{8,11},{9,10},{10,... | collective-permute-start | bytes 786440 | tf_op jit(solution)/shard_map/ppermute | solution.py:357
  28.8 2.4 %copy-start = (f32[3,256,384]{2,1,0:T(8,128)S(1)}, f32[3,256,384]{2,1,0:T(8,128)}, u32[]{:S(2)}) copy-start(f32[3,256,384]{2,1,0:T(8,128)} %constant.75.clone.refs_11_) | copy-start | bytes 3538948
  28.8 2.4 %copy-start.2 = (bf16[2,128,256]{2,1,0:T(8,128)(2,1)S(1)}, bf16[2,128,256]{2,1,0:T(8,128)(2,1)}, u32[]{:S(2)}) copy-start(bf16[2,128,256]{2,1,0:T(8,128)(2,1)} %constant.83.refs_9_) | copy-start | bytes 393220
  28.8 2.4 %copy-start.7 = (bf16[256,128]{1,0:T(8,128)(2,1)S(1)}, bf16[256,128]{1,0:T(8,128)(2,1)}, u32[]{:S(2)}) copy-start(bf16[256,128]{1,0:T(8,128)(2,1)} %constant.70.clone.refs_6_) | copy-start | bytes 196612
  28.8 2.4 %copy-start.8 = (bf16[256,128]{1,0:T(8,128)(2,1)S(1)}, bf16[256,128]{1,0:T(8,128)(2,1)}, u32[]{:S(2)}) copy-start(bf16[256,128]{1,0:T(8,128)(2,1)} %constant.69.clone.refs_5_) | copy-start | bytes 196612
  28.8 2.4 %copy-start.9 = (f32[2,24,256]{2,1,0:T(8,128)S(1)}, f32[2,24,256]{2,1,0:T(8,128)}, u32[]{:S(2)}) copy-start(f32[2,24,256]{2,1,0:T(8,128)} %constant.74.clone.refs_10_) | copy-start | bytes 147460
  31.3 19.5 %copy-start.1 = (f32[2,256,128]{2,1,0:T(8,128)S(1)}, f32[2,256,128]{2,1,0:T(8,128)}, u32[]{:S(2)}) copy-start(f32[2,256,128]{2,1,0:T(8,128)} %constant.68.clone.column_ref) | copy-start | bytes 786436
  31.3 19.5 %copy-start.3 = (bf16[4,64,256]{2,1,0:T(8,128)(2,1)S(1)}, bf16[4,64,256]{2,1,0:T(8,128)(2,1)}, u32[]{:S(2)}) copy-start(bf16[4,64,256]{2,1,0:T(8,128)(2,1)} %constant.80.clone.local_low_ref) | copy-start | bytes 393220
  31.3 19.5 %copy-start.4 = (bf16[4,64,256]{2,1,0:T(8,128)(2,1)S(1)}, bf16[4,64,256]{2,1,0:T(8,128)(2,1)}, u32[]{:S(2)}) copy-start(bf16[4,64,256]{2,1,0:T(8,128)(2,1)} %constant.79.clone.local_high_ref) | copy-start | bytes 393220
  31.3 19.5 %copy-start.5 = (bf16[256,256]{1,0:T(8,128)(2,1)S(1)}, bf16[256,256]{1,0:T(8,128)(2,1)}, u32[]{:S(2)}) copy-start(bf16[256,256]{1,0:T(8,128)(2,1)} %constant.78.clone.folded_low_ref) | copy-start | bytes 393220
  31.3 19.5 %copy-start.6 = (bf16[256,256]{1,0:T(8,128)(2,1)S(1)}, bf16[256,256]{1,0:T(8,128)(2,1)}, u32[]{:S(2)}) copy-start(bf16[256,256]{1,0:T(8,128)(2,1)} %constant.77.clone.folded_high_ref) | copy-start | bytes 393220
  31.3 19.5 %copy-start.13 = (f32[8,256]{1,0:T(8,128)S(1)}, f32[8,256]{1,0:T(8,128)}, u32[]{:S(2)}) copy-start(f32[8,256]{1,0:T(8,128)} %constant.67.clone.row_ref) | copy-start | bytes 24580
  81.6 15.7 %collective-permute-start.15 = (f32[4,64,128]{2,1,0:T(8,128)S(1)}, f32[4,64,128]{2,1,0:T(8,128)S(1)}, u32[]{:S(2)}, u32[]{:S(2)}) collective-permute-start(f32[4,64,128]{2,1,0:T(8,128)S(1)} %get-tuple-element.76), channel_id=1, source_target_pairs={{0,1},{1,0},{2,3},{3,2},{4,5},{5,4},{6,7},{7,6},{8,9},{9,8},{10,11... | collective-permute-start | bytes 393224 | tf_op jit(solution)/shard_map/ppermute | solution.py:357
  83.3 22.8 %collective-permute-start.12 = (f32[8,64,128]{2,1,0:T(8,128)S(1)}, f32[8,64,128]{2,1,0:T(8,128)S(1)}, u32[]{:S(2)}, u32[]{:S(2)}) collective-permute-start(f32[8,64,128]{2,1,0:T(8,128)S(1)} %get-tuple-element.72), channel_id=1, source_target_pairs={{0,1},{1,0},{2,3},{3,2},{4,5},{5,4},{6,7},{7,6},{8,9},{9,8},{10,11... | collective-permute-start | bytes 786440 | tf_op jit(solution)/shard_map/ppermute | solution.py:357
  83.8 24.5 %collective-permute-start.13 = (f32[8,64,128]{2,1,0:T(8,128)S(1)}, f32[8,64,128]{2,1,0:T(8,128)S(1)}, u32[]{:S(2)}, u32[]{:S(2)}) collective-permute-start(f32[8,64,128]{2,1,0:T(8,128)S(1)} %get-tuple-element.73), channel_id=1, source_target_pairs={{0,2},{1,3},{2,0},{3,1},{4,6},{5,7},{6,4},{7,5},{8,10},{9,11},{10,... | collective-permute-start | bytes 786440 | tf_op jit(solution)/shard_map/ppermute | solution.py:357
  84.3 24.6 %collective-permute-start.14 = (f32[8,64,128]{2,1,0:T(8,128)S(1)}, f32[8,64,128]{2,1,0:T(8,128)S(1)}, u32[]{:S(2)}, u32[]{:S(2)}) collective-permute-start(f32[8,64,128]{2,1,0:T(8,128)S(1)} %get-tuple-element.74), channel_id=1, source_target_pairs={{0,3},{1,2},{2,1},{3,0},{4,7},{5,6},{6,5},{7,4},{8,11},{9,10},{10,... | collective-permute-start | bytes 786440 | tf_op jit(solution)/shard_map/ppermute | solution.py:357
  85.2 11.7 %collective-permute-start.20 = (f32[8,256]{1,0:T(8,128)S(1)}, f32[8,256]{1,0:T(8,128)S(1)}, u32[]{:S(2)}, u32[]{:S(2)}) collective-permute-start(f32[8,256]{1,0:T(8,128)S(1)} %get-tuple-element.79.refs_6_), channel_id=1, source_target_pairs={{0,3},{1,2},{2,1},{3,0},{4,7},{5,6},{6,5},{7,4},{8,11},{9,10},{10,... | collective-permute-start | bytes 24584 | tf_op jit(solution)/shard_map/ppermute | solution.py:357
  96.9 6.4 %collective-permute-start.16 = (f32[4,64,128]{2,1,0:T(8,128)S(1)}, f32[4,64,128]{2,1,0:T(8,128)S(1)}, u32[]{:S(2)}, u32[]{:S(2)}) collective-permute-start(f32[4,64,128]{2,1,0:T(8,128)S(1)} %get-tuple-element.77), channel_id=1, source_target_pairs={{0,2},{1,3},{2,0},{3,1},{4,6},{5,7},{6,4},{7,5},{8,10},{9,11},{10,... | collective-permute-start | bytes 393224 | tf_op jit(solution)/shard_map/ppermute | solution.py:357
  97.4 8.3 %collective-permute-start.17 = (f32[4,64,128]{2,1,0:T(8,128)S(1)}, f32[4,64,128]{2,1,0:T(8,128)S(1)}, u32[]{:S(2)}, u32[]{:S(2)}) collective-permute-start(f32[4,64,128]{2,1,0:T(8,128)S(1)} %get-tuple-element.78), channel_id=1, source_target_pairs={{0,3},{1,2},{2,1},{3,0},{4,7},{5,6},{6,5},{7,4},{8,11},{9,10},{10,... | collective-permute-start | bytes 393224 | tf_op jit(solution)/shard_map/ppermute | solution.py:357
  103.2 10.9 %collective-permute-start.9 = (f32[4,64,128]{2,1,0:T(8,128)S(1)}, f32[4,64,128]{2,1,0:T(8,128)S(1)}, u32[]{:S(2)}, u32[]{:S(2)}) collective-permute-start(f32[4,64,128]{2,1,0:T(8,128)S(1)} %get-tuple-element.67), channel_id=1, source_target_pairs={{0,1},{1,0},{2,3},{3,2},{4,5},{5,4},{6,7},{7,6},{8,9},{9,8},{10,11... | collective-permute-start | bytes 393224 | tf_op jit(solution)/shard_map/ppermute | solution.py:357
  105.7 8.5 %collective-permute-start.10 = (f32[4,64,128]{2,1,0:T(8,128)S(1)}, f32[4,64,128]{2,1,0:T(8,128)S(1)}, u32[]{:S(2)}, u32[]{:S(2)}) collective-permute-start(f32[4,64,128]{2,1,0:T(8,128)S(1)} %get-tuple-element.68), channel_id=1, source_target_pairs={{0,2},{1,3},{2,0},{3,1},{4,6},{5,7},{6,4},{7,5},{8,10},{9,11},{10,... | collective-permute-start | bytes 393224 | tf_op jit(solution)/shard_map/ppermute | solution.py:357
  106.1 8.1 %collective-permute-start.11 = (f32[4,64,128]{2,1,0:T(8,128)S(1)}, f32[4,64,128]{2,1,0:T(8,128)S(1)}, u32[]{:S(2)}, u32[]{:S(2)}) collective-permute-start(f32[4,64,128]{2,1,0:T(8,128)S(1)} %get-tuple-element.69), channel_id=1, source_target_pairs={{0,3},{1,2},{2,1},{3,0},{4,7},{5,6},{6,5},{7,4},{8,11},{9,10},{10,... | collective-permute-start | bytes 393224 | tf_op jit(solution)/shard_map/ppermute | solution.py:357
  108.3 5.8 %collective-permute-start.19 = (f32[8,256]{1,0:T(8,128)S(1)}, f32[8,256]{1,0:T(8,128)S(1)}, u32[]{:S(2)}, u32[]{:S(2)}) collective-permute-start(f32[8,256]{1,0:T(8,128)S(1)} %get-tuple-element.79.refs_6_), channel_id=1, source_target_pairs={{0,2},{1,3},{2,0},{3,1},{4,6},{5,7},{6,4},{7,5},{8,10},{9,11},{10,... | collective-permute-start | bytes 24584 | tf_op jit(solution)/shard_map/ppermute | solution.py:357
  108.9 5.3 %collective-permute-start.18 = (f32[8,256]{1,0:T(8,128)S(1)}, f32[8,256]{1,0:T(8,128)S(1)}, u32[]{:S(2)}, u32[]{:S(2)}) collective-permute-start(f32[8,256]{1,0:T(8,128)S(1)} %get-tuple-element.79.refs_6_), channel_id=1, source_target_pairs={{0,1},{1,0},{2,3},{3,2},{4,5},{5,4},{6,7},{7,6},{8,9},{9,8},{10,11... | collective-permute-start | bytes 24584 | tf_op jit(solution)/shard_map/ppermute | solution.py:357
  (3 other events, 7.1 us)
